TPU v7x, 32 devices: a whole 2x2x4 slice. The times are simulated.
32 devices in a mesh: dp: 2 (over x), tp: 16 (over z, y, core).
Axes of the slice: x: 2, y: 2, z: 4, core: 2. Of those that a mesh axis runs over, the one named last changes fastest.
Arguments:
- x: bfloat16 [2, 4096, 2560], P('dp', 'tp'), parts along dimension 0
- ln_gain: bfloat16 [2, 2560], replicated
- ln_bias: bfloat16 [2, 2560], replicated
- w_q: bfloat16 [2, 2560, 32, 80], P(None, None, 'tp')
- b_q: bfloat16 [2, 32, 80], P(None, 'tp')
- w_k: bfloat16 [2, 2560, 32, 80], P(None, None, 'tp')
- b_k: bfloat16 [2, 32, 80], P(None, 'tp')
- w_v: bfloat16 [2, 2560, 32, 80], P(None, None, 'tp')
- b_v: bfloat16 [2, 32, 80], P(None, 'tp')
- w_o: bfloat16 [2, 32, 80, 2560], P(None, 'tp')
- b_o: bfloat16 [2, 2560], replicated
- w_up: bfloat16 [2, 2560, 10240], P(None, None, 'tp')
- b_up: bfloat16 [2, 10240], P(None, 'tp')
- w_down: bfloat16 [2, 10240, 2560], P(None, 'tp')
- b_down: bfloat16 [2, 2560], replicated
Outputs:
- output: bfloat16 [2, 4096, 2560], P('dp', 'tp'), parts along dimension 0
There are 2 independent parts. A program takes and returns all parts, laid end to end along the dimension named above; an argument that names none is the same for every part.
All inputs are finite; a program needn't handle non-finite values.
Results may differ from a plain program's by a relative error of at most 0.0175827.
Values are sent between devices in bfloat16 or wider.
A program may use at most 1 GiB of HBM per device.

v0:
```python
import jax
import jax.numpy as jnp
from jax import lax
from jax.sharding import PartitionSpec as P

ROT_DIM = 32
ROPE_BASE = 10000.0
LN_EPS = 1e-5


def rotary_tables(seq_len):
    half = ROT_DIM // 2
    inv_freq = 1.0 / (ROPE_BASE ** (jnp.arange(half, dtype=jnp.float32) * (2.0 / ROT_DIM)))
    angles = jnp.arange(seq_len, dtype=jnp.float32)[:, None] * inv_freq[None, :]
    return jnp.cos(angles), jnp.sin(angles)


def apply_rotary(projected, cosine, sine):
    half = ROT_DIM // 2
    first = projected[..., :half]
    second = projected[..., half:ROT_DIM]
    return jnp.concatenate([first * cosine - second * sine, second * cosine + first * sine, projected[..., ROT_DIM:]], axis=-1)


def layer_norm(hidden, gain, bias):
    x_f32 = hidden.astype(jnp.float32)
    mean = jnp.mean(x_f32, axis=-1, keepdims=True)
    centered = x_f32 - mean
    variance = jnp.mean(centered * centered, axis=-1, keepdims=True)
    return (centered * lax.rsqrt(variance + LN_EPS) * gain.astype(jnp.float32) + bias.astype(jnp.float32)).astype(jnp.bfloat16)


def causal_attention(q_rot, k_rot, values):
    seq_len = q_rot.shape[2]
    head_dim = q_rot.shape[3]
    scores = jnp.einsum("bhqe,bhke->bhqk", q_rot, k_rot, preferred_element_type=jnp.float32) * (head_dim ** -0.5)
    causal = jnp.arange(seq_len)[:, None] >= jnp.arange(seq_len)[None, :]
    attn_probs = jax.nn.softmax(jnp.where(causal, scores, -1e30), axis=-1).astype(jnp.bfloat16)
    return jnp.einsum("bhqk,bhke->bhqe", attn_probs, values, preferred_element_type=jnp.float32).astype(jnp.bfloat16)


def branch_partials(normed, cosine, sine, w_q, b_q, w_k, b_k, w_v, b_v, w_o, w_up, b_up, w_down):
    def project(weight, bias):
        return jnp.einsum("bld,dhe->bhle", normed, weight, preferred_element_type=jnp.float32) + bias.astype(jnp.float32)[None, :, None, :]

    q_rot = apply_rotary(project(w_q, b_q), cosine, sine).astype(jnp.bfloat16)
    k_rot = apply_rotary(project(w_k, b_k), cosine, sine).astype(jnp.bfloat16)
    values = project(w_v, b_v).astype(jnp.bfloat16)
    attended = causal_attention(q_rot, k_rot, values)
    up_act = jax.nn.gelu(jnp.einsum("bld,df->blf", normed, w_up, preferred_element_type=jnp.float32) + b_up.astype(jnp.float32), approximate=True).astype(jnp.bfloat16)
    return (jnp.einsum("bhle,hed->bld", attended, w_o, preferred_element_type=jnp.float32)
            + jnp.einsum("blf,fd->bld", up_act, w_down, preferred_element_type=jnp.float32))


def solution(mesh):
    tp_size = mesh.shape["tp"]
    head_spec = P(None, None, "tp", None)
    head_bias_spec = P(None, "tp", None)
    in_specs = (P("dp", "tp", None), P(), P(), head_spec, head_bias_spec, head_spec, head_bias_spec, head_spec, head_bias_spec,
                P(None, "tp", None, None), P(), P(None, None, "tp"), P(None, "tp"), P(None, "tp", None), P())

    def local_program(x_loc, ln_gain, ln_bias, w_q, b_q, w_k, b_k, w_v, b_v, w_o, b_o, w_up, b_up, w_down, b_down):
        cosine, sine = rotary_tables(x_loc.shape[1] * tp_size)
        hidden = x_loc
        for layer in range(w_q.shape[0]):
            normed = layer_norm(hidden, ln_gain[layer], ln_bias[layer])
            gathered = lax.all_gather(normed, "tp", axis=1, tiled=True)
            part_sum = branch_partials(gathered, cosine, sine, w_q[layer], b_q[layer], w_k[layer], b_k[layer], w_v[layer], b_v[layer],
                                       w_o[layer], w_up[layer], b_up[layer], w_down[layer]).astype(jnp.bfloat16)
            returned = lax.psum_scatter(part_sum, "tp", scatter_dimension=1, tiled=True)
            hidden = (hidden.astype(jnp.float32) + returned.astype(jnp.float32) + b_o[layer].astype(jnp.float32)
                      + b_down[layer].astype(jnp.float32)).astype(jnp.bfloat16)
        return hidden

    return jax.shard_map(local_program, mesh=mesh, in_specs=in_specs, out_specs=P("dp", "tp", None), check_vma=False)
```

profile of v0, /device:TPU:0, one launch (start us, length us, event | category | flops | bytes accessed | tf_op | source)
XLA Modules:
  0.0 1085.0 jit_solution(15536326461112027647)
XLA Ops:
  6.5 1.7 convert_reduce_fusion.1
  8.3 1.9 fusion.94
  10.2 0.7 convert_reduce_fusion.4
  10.9 1.6 fusion.97
  12.6 0.0 all-gather.3.cloned.1.call-update
  12.6 0.0 reduce-scatter.3.cloned.1.call-start
  12.7 0.6 convert_reduce_fusion.10
  13.3 0.5 bitcast_convert_fusion.1
  13.8 0.6 bitcast_convert_fusion.2
  14.4 0.6 bitcast_convert_fusion
  15.0 1.3 fusion.157
  16.3 2.4 fusion.156
  18.7 1.3 fusion.155
  20.0 1.0 fusion.133
  21.0 11.5 %iota_compare_fusion = pred[4096,4096]{0,1:T(8,128)(4,1)} fusion(), kind=kLoop, calls=%fused_computation.14 | loop fusion | flops 16777216 | bytes 16777216 | tf_op jit(solution)/shard_map/ge | solution.py:37
  32.6 91.6 %all-gather.3.cloned.1.call-done = bf16[1,4096,2560]{2,1,0:T(8,128)(2,1)} async-done(((bf16[1,256,2560]{2,1,0:T(8,128)(2,1)}), bf16[1,4096,2560]{2,1,0:T(8,128)(2,1)}) %all-gather.3.cloned.1.call-update) | async-done | bytes 20971536 | tf_op jit(solution)/shard_map/all_gather | solution.py:67
  124.2 11.1 %fusion.28 = f32[4096,160]{0,1:S(1)} fusion(bf16[2560,160]{0,1:T(8,128)(2,1)S(1)} %bitcast.235, bf16[1,4096,2560]{2,1,0:T(8,128)(2,1)} %all-gather.3.cloned.1.call-done), kind=kOutput, calls=%fused_computation.37 | convolution fusion | flops 3355443200 | bytes 24412160
  135.3 0.3 add_bitcast_fusion.3
  135.6 0.1 fusion.118
  135.7 0.7 copy-done.16
  136.4 11.4 %fusion.26 = f32[4096,160]{0,1:S(1)} fusion(bf16[2560,160]{0,1:T(8,128)(2,1)S(1)} %bitcast.234, bf16[1,4096,2560]{2,1,0:T(8,128)(2,1)} %all-gather.3.cloned.1.call-done), kind=kOutput, calls=%fused_computation.35 | convolution fusion | flops 3355443200 | bytes 24412160
  147.8 0.3 add_bitcast_fusion.2
  148.2 0.1 fusion.119
  148.3 0.3 fusion.124
  148.6 0.0 slice-start.5
  148.6 20.8 %fusion.43.clone.5 = bf16[4096,640]{1,0:T(8,128)(2,1)S(1)} fusion(bf16[1,4096,2560]{2,1,0:T(8,128)(2,1)} %all-gather.3.cloned.1.call-done, f32[640]{0:T(1024)S(1)} %get-tuple-element.14, bf16[2,2560,640]{2,1,0:T(8,128)(2,1)S(1)} %bitcast.237), kind=kOutput, calls=%fused_computation.52.clone.clone.clone.2 | convolution fusion | flops 13447987200 | bytes 29495296 | tf_op jit(solution)/shard_map/bld,df->blf/dot_general | solution.py:50
  169.4 20.6 %fusion.60 = f32[4096,2560]{1,0:T(8,128)} fusion(bf16[2,640,2560]{2,1,0:T(8,128)(2,1)S(1)} %bitcast.241, bf16[4096,640]{1,0:T(8,128)(2,1)S(1)} %fusion.43.clone.5), kind=kOutput, calls=%fused_computation.62 | convolution fusion | flops 13421772800 | bytes 50462720 | tf_op jit(solution)/shard_map/blf,fd->bld/dot_general | solution.py:52
  190.1 67.3 %fusion.158 = (f32[2,4096]{1,0:T(2,128)S(1)}, f32[2,4096,4096]{1,2,0:T(8,128)}) fusion(pred[4096,4096]{0,1:T(8,128)(4,1)} %iota_compare_fusion, bf16[2,4096,48]{1,2,0:T(8,128)(2,1)S(1)} %fusion.119, bf16[2,4096,16]{1,2,0:T(8,128)(2,1)S(1)} %get-tuple-element.33, bf16[2,4096,16]{1,2,0:T(8,128)(2,1)S(1)} %get-tuple-element.34, ...), kind=kOutput, calls=%fused_computation.194 | convolution fusion | flops 5510795264 | bytes 153649152 | tf_op jit(solution)/shard_map/sub | solution.py:38
  257.4 12.6 %fusion.24 = f32[4096,160]{0,1} fusion(bf16[2560,160]{0,1:T(8,128)(2,1)S(1)} %bitcast.233, bf16[1,4096,2560]{2,1,0:T(8,128)(2,1)} %all-gather.3.cloned.1.call-done), kind=kOutput, calls=%fused_computation.33 | convolution fusion | flops 3355443200 | bytes 24412160
  270.0 43.1 %fusion.73.clone.5 = bf16[2,4096,80]{1,2,0:T(8,128)(2,1)S(1)} fusion(f32[2,4096,4096]{1,2,0:T(8,128)} %get-tuple-element.44, f32[2,4096]{1,0:T(2,128)S(1)} %get-tuple-element.43, f32[2,80,1,4096]{3,1,0,2:T(8,128)} %bitcast.245, f32[2,80]{1,0:T(2,128)S(1)} %copy-done.33), kind=kOutput, calls=%fused_computation.74.clone.clone.clone.2 | convolution fusion | flops 5437784064 | bytes 138183296 | tf_op jit(solution)/shard_map/bhqk,bhke->bhqe/dot_general | solution.py:39
  313.2 21.1 %fusion.30 = bf16[1,4096,2560]{2,1,0:T(8,128)(2,1)} fusion(f32[4096,2560]{1,0:T(8,128)} %fusion.60, bf16[2,2,80,2560]{3,2,1,0:T(8,128)(2,1)S(1)} %copy-done.8, bf16[2,4096,80]{1,2,0:T(8,128)(2,1)S(1)} %fusion.73.clone.5), kind=kOutput, calls=%fused_computation.39 | convolution fusion | flops 3376414720 | bytes 65044480 | tf_op jit(solution)/shard_map/bhle,hed->bld/dot_general | solution.py:51
  334.2 0.0 reduce-scatter.3.cloned.1.call-update
  334.3 0.3 all-gather.5.cloned.1.call-start
  334.5 0.4 copy-done.23
  334.9 0.0 copy-done.24
  335.0 0.7 convert_reduce_fusion.2
  335.7 206.9 %reduce-scatter.3.cloned.1.call-done = bf16[1,256,2560]{2,1,0:T(8,128)(2,1)} async-done(((bf16[1,4096,2560]{2,1,0:T(8,128)(2,1)}), bf16[1,256,2560]{2,1,0:T(8,128)(2,1)}) %reduce-scatter.3.cloned.1.call-update) | async-done | bytes 1310736 | tf_op jit(solution)/shard_map/reduce_scatter | solution.py:70
  542.6 2.0 convert_reduce_fusion
  544.6 0.5 fusion.90
  545.1 0.5 copy-done.2
  545.7 1.7 fusion.93
  547.3 0.0 all-gather.5.cloned.1.call-update
  547.3 0.0 reduce-scatter.5.cloned.1.call-start
  547.4 108.1 %all-gather.5.cloned.1.call-done = bf16[1,4096,2560]{2,1,0:T(8,128)(2,1)} async-done(((bf16[1,256,2560]{2,1,0:T(8,128)(2,1)}), bf16[1,4096,2560]{2,1,0:T(8,128)(2,1)}) %all-gather.5.cloned.1.call-update) | async-done | bytes 20971536 | tf_op jit(solution)/shard_map/all_gather | solution.py:67
  655.5 11.1 %fusion.20 = f32[4096,160]{0,1:S(1)} fusion(bf16[2560,160]{0,1:T(8,128)(2,1)S(1)} %bitcast.232, bf16[1,4096,2560]{2,1,0:T(8,128)(2,1)} %all-gather.5.cloned.1.call-done), kind=kOutput, calls=%fused_computation.29 | convolution fusion | flops 3355443200 | bytes 24412160
  666.6 0.3 add_bitcast_fusion.1
  666.9 0.1 fusion.120
  667.0 0.7 copy-done.13
  667.7 11.4 %fusion.18 = f32[4096,160]{0,1:S(1)} fusion(bf16[2560,160]{0,1:T(8,128)(2,1)S(1)} %bitcast.231, bf16[1,4096,2560]{2,1,0:T(8,128)(2,1)} %all-gather.5.cloned.1.call-done), kind=kOutput, calls=%fused_computation.27 | convolution fusion | flops 3355443200 | bytes 24412160
  679.2 0.3 add_bitcast_fusion
  679.5 0.6 copy-done.5
  680.1 0.1 copy-done.7
  680.2 0.3 fusion.128
  680.4 0.1 fusion.121
  680.5 0.3 copy-done.26
  680.8 21.1 %fusion.51.clone.5 = bf16[4096,640]{1,0:T(8,128)(2,1)S(1)} fusion(bf16[1,4096,2560]{2,1,0:T(8,128)(2,1)} %all-gather.5.cloned.1.call-done, f32[640]{0:T(1024)S(1)} %copy-done.26, bf16[2,2560,640]{2,1,0:T(8,128)(2,1)S(1)} %bitcast.239), kind=kOutput, calls=%fused_computation.60.clone.clone.clone.2 | convolution fusion | flops 13447987200 | bytes 29495296 | tf_op jit(solution)/shard_map/bld,df->blf/dot_general | solution.py:50
  701.9 20.8 %fusion.57 = f32[4096,2560]{1,0:T(8,128)} fusion(bf16[2,640,2560]{2,1,0:T(8,128)(2,1)S(1)} %bitcast.243, bf16[4096,640]{1,0:T(8,128)(2,1)S(1)} %fusion.51.clone.5), kind=kOutput, calls=%fused_computation.61 | convolution fusion | flops 13421772800 | bytes 50462720 | tf_op jit(solution)/shard_map/blf,fd->bld/dot_general | solution.py:52
  722.8 67.3 %fusion.159 = (f32[2,4096]{1,0:T(2,128)S(1)}, f32[2,4096,4096]{1,2,0:T(8,128)}) fusion(pred[4096,4096]{0,1:T(8,128)(4,1)} %iota_compare_fusion, bf16[2,4096,48]{1,2,0:T(8,128)(2,1)S(1)} %fusion.121, bf16[2,4096,16]{1,2,0:T(8,128)(2,1)S(1)} %get-tuple-element.31, bf16[2,4096,16]{1,2,0:T(8,128)(2,1)S(1)} %get-tuple-element.32, ...), kind=kOutput, calls=%fused_computation.195 | convolution fusion | flops 5510795264 | bytes 153649152 | tf_op jit(solution)/shard_map/sub | solution.py:38
  790.1 12.6 %fusion.16 = f32[4096,160]{0,1} fusion(bf16[2560,160]{0,1:T(8,128)(2,1)S(1)} %bitcast.230, bf16[1,4096,2560]{2,1,0:T(8,128)(2,1)} %all-gather.5.cloned.1.call-done), kind=kOutput, calls=%fused_computation.25 | convolution fusion | flops 3355443200 | bytes 24412160
  802.7 43.1 %fusion.72.clone.5 = bf16[2,4096,80]{1,2,0:T(8,128)(2,1)S(1)} fusion(f32[2,4096,4096]{1,2,0:T(8,128)} %get-tuple-element.46, f32[2,4096]{1,0:T(2,128)S(1)} %get-tuple-element.45, f32[2,80,1,4096]{3,1,0,2:T(8,128)} %bitcast.244, f32[2,80]{1,0:T(2,128)S(1)} %copy-done.32), kind=kOutput, calls=%fused_computation.73.clone.clone.clone.2 | convolution fusion | flops 5437784064 | bytes 138183296 | tf_op jit(solution)/shard_map/bhqk,bhke->bhqe/dot_general | solution.py:39
  845.9 21.1 %fusion.31 = bf16[1,4096,2560]{2,1,0:T(8,128)(2,1)} fusion(f32[4096,2560]{1,0:T(8,128)} %fusion.57, bf16[2,2,80,2560]{3,2,1,0:T(8,128)(2,1)S(1)} %copy-done.9, bf16[2,4096,80]{1,2,0:T(8,128)(2,1)S(1)} %fusion.72.clone.5), kind=kOutput, calls=%fused_computation.40 | convolution fusion | flops 3376414720 | bytes 65044480 | tf_op jit(solution)/shard_map/bhle,hed->bld/dot_general | solution.py:51
  866.9 0.0 reduce-scatter.5.cloned.1.call-update
  867.0 208.2 %reduce-scatter.5.cloned.1.call-done = bf16[1,256,2560]{2,1,0:T(8,128)(2,1)} async-done(((bf16[1,4096,2560]{2,1,0:T(8,128)(2,1)}), bf16[1,256,2560]{2,1,0:T(8,128)(2,1)}) %reduce-scatter.5.cloned.1.call-update) | async-done | bytes 1310736 | tf_op jit(solution)/shard_map/reduce_scatter | solution.py:70
  1075.2 2.8 fusion.103
  (85 shorter events, 0.2 us)
Async XLA Ops:
  6.5 4.4 copy-start
  6.5 3.7 copy-start.22
  6.5 3.7 copy-start.21
  6.5 117.6 %all-gather.3.cloned.1.call-start = ((), (), s32[]{:S(2)}) async-start(), calls=%async_computation.2 | async-start | bytes 22282240 | tf_op jit(solution)/shard_map/all_gather | solution.py:67
  8.2 4.4 copy-start.25
  8.2 5.0 copy-start.29
  8.2 5.6 copy-start.30
  8.3 6.1 copy-start.31
  8.3 6.7 copy-start.10
  12.6 530.0 %reduce-scatter.3.cloned.1.call-start = ((), (), s32[]{:S(2)}) async-start(), calls=%async_computation.3 | async-start | bytes 22282240 | tf_op jit(solution)/shard_map/reduce_scatter | solution.py:70
  15.0 3.7 copy-start.11
  21.0 127.3 %copy-start.4 = (f32[4096,16]{0,1:T(8,128)}, f32[4096,16]{0,1:T(8,128)S(1)}, u32[]{:S(2)}) copy-start(f32[4096,16]{0,1:T(8,128)S(1)} %get-tuple-element.41) | copy-start | bytes 786436
  21.0 127.3 %copy-start.6 = (f32[4096,16]{0,1:T(8,128)}, f32[4096,16]{0,1:T(8,128)S(1)}, u32[]{:S(2)}) copy-start(f32[4096,16]{0,1:T(8,128)S(1)} %get-tuple-element.42) | copy-start | bytes 786436
  135.2 1.1 copy-start.16
  135.6 13.0 %slice-start = ((s8[6553600]{0:T(1024)(128)(4,1)}), s8[4194304]{0:T(1024)(128)(4,1)S(1)}, s32[]{:S(2)}) async-start(s8[6553600]{0:T(1024)(128)(4,1)} %bitcast.236), calls=%async_computation.6 | async-start | bytes 8388608
  136.4 12.2 %slice-start.1 = ((s8[6553600]{0:T(1024)(128)(4,1)}), s8[2359296]{0:T(1024)(128)(4,1)S(1)}, s32[]{:S(2)}) async-start(s8[6553600]{0:T(1024)(128)(4,1)} %bitcast.236), calls=%async_computation.7 | async-start | bytes 4718592
  148.3 21.1 %slice-start.4 = ((s8[6553600]{0:T(1024)(128)(4,1)}), s8[4194304]{0:T(1024)(128)(4,1)S(1)}, s32[]{:S(2)}) async-start(s8[6553600]{0:T(1024)(128)(4,1)} %bitcast.240), calls=%async_computation.10 | async-start | bytes 8388608
  148.6 20.8 %slice-start.5 = ((s8[6553600]{0:T(1024)(128)(4,1)}), s8[2359296]{0:T(1024)(128)(4,1)S(1)}, s32[]{:S(2)}) async-start(s8[6553600]{0:T(1024)(128)(4,1)} %bitcast.240), calls=%async_computation.11 | async-start | bytes 4718592
  190.1 67.3 %copy-start.15 = (bf16[1,2560,2,80]{1,3,2,0:T(8,128)(2,1)S(1)}, bf16[1,2560,2,80]{1,3,2,0:T(8,128)(2,1)}, u32[]{:S(2)}) copy-start(bf16[1,2560,2,80]{1,3,2,0:T(8,128)(2,1)} %get-tuple-element.26) | copy-start | bytes 2457604
  257.4 12.7 %copy-start.33 = (f32[2,80]{1,0:T(2,128)S(1)}, f32[2,80]{1,0:T(2,128)}, u32[]{:S(2)}) copy-start(f32[2,80]{1,0:T(2,128)} %get-tuple-element.36) | copy-start | bytes 1924
  270.0 43.1 %copy-start.8 = (bf16[2,2,80,2560]{3,2,1,0:T(8,128)(2,1)S(1)}, bf16[2,2,80,2560]{3,2,1,0:T(8,128)(2,1)}, u32[]{:S(2)}) copy-start(bf16[2,2,80,2560]{3,2,1,0:T(8,128)(2,1)} %param.24) | copy-start | bytes 4915204
  334.2 0.7 copy-start.23
  334.2 0.7 copy-start.24
  334.2 208.3 %copy-start.1 = (bf16[1,256,2560]{2,1,0:T(8,128)(2,1)S(1)}, bf16[1,256,2560]{2,1,0:T(8,128)(2,1)}, u32[]{:S(2)}) copy-start(bf16[1,256,2560]{2,1,0:T(8,128)(2,1)} %param.15) | copy-start | bytes 3932164
  334.3 321.2 %all-gather.5.cloned.1.call-start = ((), (), s32[]{:S(2)}) async-start(), calls=%async_computation.4 | async-start | bytes 22282240 | tf_op jit(solution)/shard_map/all_gather | solution.py:67
  542.6 3.1 copy-start.17
  542.6 3.1 copy-start.18
  544.6 1.1 copy-start.2
  544.6 110.9 %copy-start.14 = (bf16[1,2560,2,80]{1,3,2,0:T(8,128)(2,1)S(1)}, bf16[1,2560,2,80]{1,3,2,0:T(8,128)(2,1)}, u32[]{:S(2)}) copy-start(bf16[1,2560,2,80]{1,3,2,0:T(8,128)(2,1)} %get-tuple-element.27) | copy-start | bytes 2457604
  547.3 527.8 %reduce-scatter.5.cloned.1.call-start = ((), (), s32[]{:S(2)}) async-start(), calls=%async_computation.5 | async-start | bytes 22282240 | tf_op jit(solution)/shard_map/reduce_scatter | solution.py:70
  655.5 11.1 %copy-start.28 = (f32[2,80]{1,0:T(2,128)S(1)}, f32[2,80]{1,0:T(2,128)}, u32[]{:S(2)}) copy-start(f32[2,80]{1,0:T(2,128)} %get-tuple-element.37) | copy-start | bytes 1924
  666.6 1.1 copy-start.13
  666.6 14.0 %slice-start.2 = ((s8[6553600]{0:T(1024)(128)(4,1)}), s8[4194304]{0:T(1024)(128)(4,1)S(1)}, s32[]{:S(2)}) async-start(s8[6553600]{0:T(1024)(128)(4,1)} %bitcast.238), calls=%async_computation.8 | async-start | bytes 8388608
  667.7 11.4 %copy-start.27 = (f32[2,80]{1,0:T(2,128)S(1)}, f32[2,80]{1,0:T(2,128)}, u32[]{:S(2)}) copy-start(f32[2,80]{1,0:T(2,128)} %get-tuple-element.39) | copy-start | bytes 1924
  667.7 12.8 %slice-start.3 = ((s8[6553600]{0:T(1024)(128)(4,1)}), s8[2359296]{0:T(1024)(128)(4,1)S(1)}, s32[]{:S(2)}) async-start(s8[6553600]{0:T(1024)(128)(4,1)} %bitcast.238), calls=%async_computation.9 | async-start | bytes 4718592
  679.1 1.0 copy-start.5
  679.1 1.0 copy-start.7
  680.2 0.7 copy-start.26
  680.2 21.8 %slice-start.6 = ((s8[6553600]{0:T(1024)(128)(4,1)}), s8[4194304]{0:T(1024)(128)(4,1)S(1)}, s32[]{:S(2)}) async-start(s8[6553600]{0:T(1024)(128)(4,1)} %bitcast.242), calls=%async_computation.12 | async-start | bytes 8388608
  680.8 21.1 %slice-start.7 = ((s8[6553600]{0:T(1024)(128)(4,1)}), s8[2359296]{0:T(1024)(128)(4,1)S(1)}, s32[]{:S(2)}) async-start(s8[6553600]{0:T(1024)(128)(4,1)} %bitcast.242), calls=%async_computation.13 | async-start | bytes 4718592
  722.8 67.3 %copy-start.12 = (bf16[1,2560,2,80]{1,3,2,0:T(8,128)(2,1)S(1)}, bf16[1,2560,2,80]{1,3,2,0:T(8,128)(2,1)}, u32[]{:S(2)}) copy-start(bf16[1,2560,2,80]{1,3,2,0:T(8,128)(2,1)} %get-tuple-element.25) | copy-start | bytes 2457604
  790.1 12.6 %copy-start.32 = (f32[2,80]{1,0:T(2,128)S(1)}, f32[2,80]{1,0:T(2,128)}, u32[]{:S(2)}) copy-start(f32[2,80]{1,0:T(2,128)} %get-tuple-element.35) | copy-start | bytes 1924
  802.7 43.1 %copy-start.9 = (bf16[2,2,80,2560]{3,2,1,0:T(8,128)(2,1)S(1)}, bf16[2,2,80,2560]{3,2,1,0:T(8,128)(2,1)}, u32[]{:S(2)}) copy-start(bf16[2,2,80,2560]{3,2,1,0:T(8,128)(2,1)} %param.24) | copy-start | bytes 4915204
  866.9 208.3 %copy-start.3 = (bf16[1,256,2560]{2,1,0:T(8,128)(2,1)S(1)}, bf16[1,256,2560]{2,1,0:T(8,128)(2,1)}, u32[]{:S(2)}) copy-start(bf16[1,256,2560]{2,1,0:T(8,128)(2,1)} %copy-done.2) | copy-start | bytes 3932164
  866.9 208.3 %copy-start.19 = (f32[2560]{0:T(1024)S(1)}, f32[2560]{0:T(1024)}, u32[]{:S(2)}) copy-start(f32[2560]{0:T(1024)} %get-tuple-element.7) | copy-start | bytes 30724
  866.9 208.3 %copy-start.20 = (f32[2560]{0:T(1024)S(1)}, f32[2560]{0:T(1024)}, u32[]{:S(2)}) copy-start(f32[2560]{0:T(1024)} %get-tuple-element.50) | copy-start | bytes 30724
Sparse Core Ops, SparseCore 0:
  12.7 111.4 all-gather.2
  334.4 208.1 reduce-scatter.2
  547.5 107.9 all-gather.4
  867.1 208.0 reduce-scatter.4
where the time goes:
time: 1090 us
  waiting for transfers between devices  615 us (56%)
  matrix products  417 us (38%)
  other arithmetic  30.3 us (3%)
  between operations  14.1 us (1%)
    reduce_scatter x2, waiting for transfers between devices, local_program(): returned = lax.psum_scatter(part_sum, 'tp', scatter_dimension=1, tiled=True)  415 us
    all_gather x2, waiting for transfers between devices, local_program(): gathered = lax.all_gather(normed, 'tp', axis=1, tiled=True)  200 us
    sub x2, matrix products, causal_attention(): jax.nn.softmax(jnp.where(causal, scores, -1e+30), axis=-1)  135 us
    dot_general x2, matrix products, causal_attention(): jnp.einsum('bhqk,bhke->bhqe', attn_probs, values, preferred_element_type=...  86.2 us
    unnamed x6, matrix products  70.2 us
    dot_general x2, matrix products, branch_partials(): jnp.einsum('bhle,hed->bld', attended, w_o, preferred_element_type=jnp.flo...  42.1 us
    dot_general x2, matrix products, branch_partials(): jnp.einsum('bld,df->blf', normed, w_up, preferred_element_type=jnp.float32)  41.9 us
    dot_general x2, matrix products, branch_partials(): jnp.einsum('blf,fd->bld', up_act, w_down, preferred_element_type=jnp.floa...  41.5 us
  transfers between devices with their start and end apart: 4, of which 4 were waited for; matrix products, arithmetic and copies ran while one was open for 2% of the time, Pallas kernels for 0%

commit v1 on v0

v1 whole, which is shorter than its diff:
```python
import functools

import jax
import jax.numpy as jnp
from jax import lax
from jax.experimental import pallas as pl
from jax.experimental.pallas import tpu as pltpu
from jax.sharding import PartitionSpec as P

ROT_DIM = 32
ROPE_BASE = 10000.0
LN_EPS = 1e-5
LANES = 128
RING = 8
LOG2_E = 1.4426950408889634
MESH = pl.DeviceIdType.MESH
VMEM_LIMIT = 62 * 1024 * 1024
F32 = jnp.float32
BF16 = jnp.bfloat16


def ring_to_chip(pos):
    y = ((pos + 3) // 4) % 2
    z = y * (pos - 1) + (1 - y) * ((RING - pos) % RING)
    return 2 * z + y


def chip_to_ring(chip):
    y = chip % 2
    z = chip // 2
    return y * (z + 1) + (1 - y) * ((RING - z) % RING)


def place():
    me = lax.axis_index("tp")
    core = me % 2
    chip = me // 2
    pos = chip_to_ring(chip)
    right = 2 * ring_to_chip((pos + 1) % RING) + core
    left = 2 * ring_to_chip((pos + RING - 1) % RING) + core
    partner = 2 * chip + (1 - core)
    return core, chip, pos, right, left, partner


def meet(right, left, partner):
    barrier = pltpu.get_barrier_semaphore()
    for other in (right, left, partner):
        pl.semaphore_signal(barrier, inc=1, device_id={"tp": other}, device_id_type=MESH)
    pl.semaphore_wait(barrier, 3)


def layer_norm(hidden, gain, bias):
    x_f32 = hidden.astype(F32)
    mean = jnp.mean(x_f32, axis=-1, keepdims=True)
    centered = x_f32 - mean
    variance = jnp.mean(centered * centered, axis=-1, keepdims=True)
    return (centered * lax.rsqrt(variance + LN_EPS) * gain.astype(F32) + bias.astype(F32)).astype(BF16)


def gather_kernel(h_hbm, w_qkv, w_up, b_qkv, b_up, cos_t, sin_t, q_out, k_out, v_out, m_out,
                  hbuf, local_sem, ring_send, ring_recv, pair_send, pair_recv):
    half = hbuf.shape[2] // 2
    piece = half // 2
    core, chip, pos, right, left, partner = place()
    meet(right, left, partner)

    def block(way, step):
        return ring_to_chip((pos + (RING - step if way == 0 else step)) % RING)

    def rows_of(way, step, part, side):
        return hbuf.at[way, block(way, step), pl.ds(side * half + part * piece, piece)]

    def ring_copy(way, step, part):
        ref = rows_of(way, step, part, core)
        return pltpu.make_async_remote_copy(
            src_ref=ref, dst_ref=ref, send_sem=ring_send.at[way, step, part], recv_sem=ring_recv.at[way, step, part],
            device_id={"tp": right if way == 0 else left}, device_id_type=MESH)

    def ring_arrival(way, step, part):
        ref = rows_of(way, step, part, core)
        return pltpu.make_async_remote_copy(
            src_ref=ref, dst_ref=ref, send_sem=ring_send.at[way, step - 1, part], recv_sem=ring_recv.at[way, step - 1, part],
            device_id={"tp": right if way == 0 else left}, device_id_type=MESH)

    def pair_copy(way, step, part, side):
        ref = rows_of(way, step, part, side)
        return pltpu.make_async_remote_copy(
            src_ref=ref, dst_ref=ref, send_sem=pair_send.at[way, step, part], recv_sem=pair_recv.at[way, step, part],
            device_id={"tp": partner}, device_id_type=MESH)

    def own_copy(way):
        return pltpu.make_async_copy(h_hbm.at[pl.ds(way * half, half)],
                                     hbuf.at[way, chip, pl.ds(core * half, half)], local_sem.at[way])

    for way in range(2):
        own_copy(way).start()
    for way in range(2):
        own_copy(way).wait()
        for part in range(2):
            ring_copy(way, 0, part).start()
            pair_copy(way, 0, part, core).start()

    def rotate(value, cosine, sine):
        lane = lax.broadcasted_iota(jnp.int32, value.shape, 1)
        swapped = jnp.where(lane < ROT_DIM // 2, pltpu.roll(value, LANES - ROT_DIM // 2, 1), pltpu.roll(value, ROT_DIM // 2, 1))
        return value * cosine + swapped * sine

    def compute(way, step):
        for part in range(2):
            pair_copy(way, step, part, 1 - core).wait_recv()
        at = block(way, step)
        normed = hbuf[way, at]
        cosine, sine = cos_t[at, way], sin_t[at, way]
        width = w_qkv.shape[1] // 3
        for which, out in enumerate((q_out, k_out, v_out)):
            cols = slice(which * width, (which + 1) * width)
            proj = jnp.dot(normed, w_qkv[:, cols], preferred_element_type=F32) + b_qkv[:, cols]
            if which < 2:
                for head in range(width // LANES):
                    lanes = slice(head * LANES, (head + 1) * LANES)
                    out[at, way, :, lanes] = rotate(proj[:, lanes], cosine, sine).astype(BF16)
            else:
                out[at, way] = proj.astype(BF16)
        up = jnp.dot(normed, w_up[...], preferred_element_type=F32) + b_up[...]
        m_out[at, way] = jax.nn.gelu(up, approximate=True).astype(BF16)

    def step_body(step, carry):
        for part in range(2):
            for way in range(2):
                ring_arrival(way, step, part).wait_recv()

                @pl.when(step < RING - 1)
                def _():
                    ring_copy(way, step, part).start()

                pair_copy(way, step, part, core).start()
            compute(part, step - 1)
        return carry

    lax.fori_loop(1, RING, step_body, 0)
    for way in range(2):
        compute(way, RING - 1)

    def drain(step, carry):
        for way in range(2):
            for part in range(2):
                @pl.when(step < RING - 1)
                def _():
                    ring_copy(way, step, part).wait_send()

                pair_copy(way, step, part, core).wait_send()
        return carry

    lax.fori_loop(0, RING, drain, 0)


def gather_project(h, w_qkv, w_up, b_qkv, b_up, cos_t, sin_t, collective_id):
    rows, depth = h.shape
    qkv_shape = jax.ShapeDtypeStruct((RING, 2, rows, w_qkv.shape[1] // 3), BF16)
    m_shape = jax.ShapeDtypeStruct((RING, 2, rows, w_up.shape[1]), BF16)
    vmem = pl.BlockSpec(memory_space=pltpu.VMEM)
    return pl.pallas_call(
        gather_kernel,
        out_shape=(qkv_shape, qkv_shape, qkv_shape, m_shape),
        in_specs=[pl.BlockSpec(memory_space=pl.ANY)] + [vmem] * 6,
        out_specs=(vmem,) * 4,
        scratch_shapes=[
            pltpu.VMEM((2, RING, rows, depth), BF16),
            pltpu.SemaphoreType.DMA((2,)),
            pltpu.SemaphoreType.DMA((2, RING, 2)),
            pltpu.SemaphoreType.DMA((2, RING, 2)),
            pltpu.SemaphoreType.DMA((2, RING, 2)),
            pltpu.SemaphoreType.DMA((2, RING, 2)),
        ],
        compiler_params=pltpu.CompilerParams(collective_id=collective_id, has_side_effects=True, vmem_limit_bytes=VMEM_LIMIT),
        name=f"gather_project_{collective_id}",
    )(h, w_qkv, w_up, b_qkv, b_up, cos_t, sin_t)


def scatter_kernel(last, head_dim, q_ref, k_ref, v_ref, m_ref, w_o, w_down, x_ref, b_o, b_down, gain, bias, *refs):
    if last:
        hid_out, h_out = refs[0], None
        refs = refs[1:]
    else:
        hid_out, h_out = refs[0], refs[1]
        refs = refs[2:]
    acc, top, held, given, taken, own, ring_send, ring_recv, pair_send, pair_recv = refs
    rows = q_ref.shape[2]
    half = rows // 2
    piece = half // 2
    depth = w_o.shape[1]
    heads = q_ref.shape[3] // LANES
    tile = next(t for t in (512, 256, 128) if depth % t == 0)
    scale = head_dim ** -0.5 * LOG2_E
    core, chip, pos, right, left, partner = place()
    mine, other = pl.ds(core * half, half), pl.ds((1 - core) * half, half)

    for way in range(2):
        held[way, 0] = jnp.zeros((half, depth), BF16)
    meet(right, left, partner)

    def block(way, step):
        return ring_to_chip((pos + (2 * RING - 1 - step if way == 0 else 1 + step)) % RING)

    def ring_copy(way, step, part):
        span = pl.ds(part * piece, piece)
        return pltpu.make_async_remote_copy(
            src_ref=held.at[way, step, span], dst_ref=held.at[way, step + 1, span],
            send_sem=ring_send.at[way, step, part], recv_sem=ring_recv.at[way, step, part],
            device_id={"tp": right if way == 0 else left}, device_id_type=MESH)

    def pair_copy(way, step):
        return pltpu.make_async_remote_copy(
            src_ref=given.at[way, step % 2], dst_ref=taken.at[way, step],
            send_sem=pair_send.at[way, step], recv_sem=pair_recv.at[way, step],
            device_id={"tp": partner}, device_id_type=MESH)

    def attend(way, at):
        row = lax.broadcasted_iota(jnp.int32, (rows, 1), 0)
        row_side = (row // half + core) % 2
        row_pos = row_side * (2 * half) + way * half + row % half
        col = lax.broadcasted_iota(jnp.int32, (1, 2 * rows), 1)
        col_pos = ((col // half) % 2) * (2 * half) + (col // rows) * half + col % half
        queries = []
        for head in range(heads):
            lanes = slice(head * LANES, (head + 1) * LANES)
            queries.append(jnp.concatenate([q_ref[at, way, mine, lanes], q_ref[at, way, other, lanes]], axis=0))
            keys = k_ref[at, :, :, lanes].reshape(2 * rows, LANES)
            values = v_ref[at, :, :, lanes].reshape(2 * rows, LANES)
            score = lax.dot_general(queries[head], keys, (((1,), (1,)), ((), ())), preferred_element_type=F32) * scale
            score = jnp.where(row_pos >= col_pos, score, -1e30)
            peak = jnp.max(score, axis=1, keepdims=True)
            prob = jnp.exp2(score - peak).astype(BF16)
            acc[head] = jnp.dot(prob, values, preferred_element_type=F32)
            top[head] = jnp.broadcast_to(peak, (rows, LANES))

        def body(earlier, carry):
            for head in range(heads):
                lanes = slice(head * LANES, (head + 1) * LANES)
                keys = k_ref[earlier, :, :, lanes].reshape(2 * rows, LANES)
                values = v_ref[earlier, :, :, lanes].reshape(2 * rows, LANES)
                score = lax.dot_general(queries[head], keys, (((1,), (1,)), ((), ())), preferred_element_type=F32) * scale
                before = top[head][:, :1]
                peak = jnp.maximum(before, jnp.max(score, axis=1, keepdims=True))
                prob = jnp.exp2(score - peak).astype(BF16)
                acc[head] = acc[head] * jnp.exp2(before - peak) + jnp.dot(prob, values, preferred_element_type=F32)
                top[head] = jnp.broadcast_to(peak, (rows, LANES))
            return carry

        lax.fori_loop(0, at, body, 0)
        done = [(acc[head] / acc[head][:, head_dim:head_dim + 1]).astype(BF16) for head in range(heads)]
        return jnp.concatenate(done, axis=1)

    def compute(way, step):
        at = block(way, step)
        attended = attend(way, at)
        up = jnp.concatenate([m_ref[at, way, mine], m_ref[at, way, other]], axis=0)

        @pl.when(step >= 2)
        def _():
            pair_copy(way, step - 2).wait_send()

        for low in range(0, depth, tile):
            cols = slice(low, low + tile)
            part_sum = (jnp.dot(attended, w_o[:, cols], preferred_element_type=F32)
                        + jnp.dot(up, w_down[:, cols], preferred_element_type=F32))
            own[way, step % 2, :, cols] = part_sum[:half]
            given[way, step % 2, :, cols] = part_sum[half:].astype(BF16)
        pair_copy(way, step).start()

    def total(way, step, part):
        span = pl.ds(part * piece, piece)
        return (own[way, step % 2, span] + taken[way, step, span].astype(F32) + held[way, step, span].astype(F32))

    for way in range(2):
        compute(way, 0)

    def step_body(step, carry):
        for part in range(2):
            for way in range(2):
                if part == 0:
                    pair_copy(way, step).wait_recv()

                @pl.when(step > 0)
                def _():
                    ring_copy(way, step - 1, part).wait_recv()

                held[way, step, pl.ds(part * piece, piece)] = total(way, step, part).astype(BF16)
                ring_copy(way, step, part).start()
            compute(part, step + 1)
        return carry

    lax.fori_loop(0, RING - 1, step_body, 0)
    for part in range(2):
        for way in range(2):
            if part == 0:
                pair_copy(way, RING - 1).wait_recv()
            ring_copy(way, RING - 2, part).wait_recv()
            span = pl.ds(way * half + part * piece, piece)
            hidden = (x_ref[span].astype(F32) + total(way, RING - 1, part) + b_o[...] + b_down[...]).astype(BF16)
            hid_out[span] = hidden
            if h_out is not None:
                h_out[span] = layer_norm(hidden, gain[...], bias[...])

    def drain(step, carry):
        for way in range(2):
            for part in range(2):
                ring_copy(way, step, part).wait_send()
        return carry

    lax.fori_loop(0, RING - 1, drain, 0)
    for way in range(2):
        for step in (RING - 2, RING - 1):
            pair_copy(way, step).wait_send()


def attend_scatter(q, k, v, m, w_o, w_down, x, b_o, b_down, gain, bias, head_dim, last, collective_id):
    rows, depth = x.shape
    half = rows // 2
    heads = q.shape[3] // LANES
    shape = jax.ShapeDtypeStruct((rows, depth), BF16)
    vmem = pl.BlockSpec(memory_space=pltpu.VMEM)
    outs = 1 if last else 2
    return pl.pallas_call(
        functools.partial(scatter_kernel, last, head_dim),
        out_shape=(shape,) * outs,
        in_specs=[vmem] * 11,
        out_specs=(vmem,) * outs,
        scratch_shapes=[
            pltpu.VMEM((heads, rows, LANES), F32),
            pltpu.VMEM((heads, rows, LANES), F32),
            pltpu.VMEM((2, RING, half, depth), BF16),
            pltpu.VMEM((2, 2, half, depth), BF16),
            pltpu.VMEM((2, RING, half, depth), BF16),
            pltpu.VMEM((2, 2, half, depth), F32),
            pltpu.SemaphoreType.DMA((2, RING, 2)),
            pltpu.SemaphoreType.DMA((2, RING, 2)),
            pltpu.SemaphoreType.DMA((2, RING)),
            pltpu.SemaphoreType.DMA((2, RING)),
        ],
        compiler_params=pltpu.CompilerParams(collective_id=collective_id, has_side_effects=True, vmem_limit_bytes=VMEM_LIMIT),
        name=f"attend_scatter_{collective_id}",
    )(q, k, v, m, w_o, w_down, x, b_o, b_down, gain, bias)


def rotary_tables(rows):
    half = rows // 2
    chip, way, core, row = jnp.meshgrid(jnp.arange(RING), jnp.arange(2), jnp.arange(2), jnp.arange(half), indexing="ij")
    position = (chip * (2 * rows) + core * rows + way * half + row).astype(F32).reshape(RING, 2, rows, 1)
    pairs = ROT_DIM // 2
    inv_freq = 1.0 / (ROPE_BASE ** (jnp.arange(pairs, dtype=F32) * (2.0 / ROT_DIM)))
    angles = position * inv_freq
    cosine, sine = jnp.cos(angles), jnp.sin(angles)
    rest = (RING, 2, rows, LANES - ROT_DIM)
    return (jnp.concatenate([cosine, cosine, jnp.ones(rest, F32)], axis=-1),
            jnp.concatenate([-sine, sine, jnp.zeros(rest, F32)], axis=-1))


def solution(mesh):
    head_spec = P(None, None, "tp", None)
    head_bias_spec = P(None, "tp", None)
    in_specs = (P("dp", "tp", None), P(), P(), head_spec, head_bias_spec, head_spec, head_bias_spec, head_spec, head_bias_spec,
                P(None, "tp", None, None), P(), P(None, None, "tp"), P(None, "tp"), P(None, "tp", None), P())

    def local_program(x_loc, ln_gain, ln_bias, w_q, b_q, w_k, b_k, w_v, b_v, w_o, b_o, w_up, b_up, w_down, b_down):
        hidden = x_loc[0]
        rows, depth = hidden.shape
        layers, _, heads, head_dim = w_q.shape
        spare = LANES - head_dim
        cos_t, sin_t = rotary_tables(rows)

        def pad_in(weight):
            return jnp.pad(weight, ((0, 0), (0, 0), (0, spare))).reshape(depth, heads * LANES)

        def pad_bias(vector, one):
            padded = jnp.pad(vector.astype(F32), ((0, 0), (0, spare)))
            if one:
                padded = padded.at[:, head_dim].set(1.0)
            return padded.reshape(1, heads * LANES)

        def row(vector):
            return vector.astype(F32).reshape(1, -1)

        normed = layer_norm(hidden, ln_gain[0], ln_bias[0])
        for layer in range(layers):
            last = layer == layers - 1
            w_qkv = jnp.concatenate([pad_in(w_q[layer]), pad_in(w_k[layer]), pad_in(w_v[layer])], axis=1)
            b_qkv = jnp.concatenate([pad_bias(b_q[layer], False), pad_bias(b_k[layer], False), pad_bias(b_v[layer], True)], axis=1)
            w_out = jnp.pad(w_o[layer], ((0, 0), (0, spare), (0, 0))).reshape(heads * LANES, depth)
            q, k, v, m = gather_project(normed, w_qkv, w_up[layer], b_qkv, row(b_up[layer]), cos_t, sin_t, 2 * layer)
            after = 0 if last else layer + 1
            results = attend_scatter(q, k, v, m, w_out, w_down[layer], hidden, row(b_o[layer]), row(b_down[layer]),
                                     row(ln_gain[after]), row(ln_bias[after]), head_dim, last, 2 * layer + 1)
            hidden = results[0]
            normed = None if last else results[1]
        return hidden[None]

    return jax.shard_map(local_program, mesh=mesh, in_specs=in_specs, out_specs=P("dp", "tp", None), check_vma=False)
```

time: 1090 us -> 581 us (0.53)
  waiting for transfers between devices: 615 us -> 0 us
  Pallas kernels: 0 us -> 513 us
  matrix products: 417 us -> 0 us
  local copies, waits for them, and re-layouts: 8.89 us -> 34.9 us
  between operations: 14.1 us -> 1.29 us
    pallas_call x0 -> x4, Pallas kernels: none -> 513 us  [the longest x2 272 us: attend_scatter(): pl.pallas_call(functools.partial(scatter_kernel, last, head_dim), out_sha...]
    reduce_scatter x2 -> x0, waiting for transfers between devices: 415 us -> none  [local_program(): returned = lax.psum_scatter(part_sum, 'tp', scatter_dimension=1, tiled=True)]
    dot_general x8 -> x0, matrix products: 212 us -> none  [the longest x2 86.2 us: causal_attention(): jnp.einsum('bhqk,bhke->bhqe', attn_probs, values, preferred_element_type=...]
    all_gather x2 -> x0, waiting for transfers between devices: 200 us -> none  [local_program(): gathered = lax.all_gather(normed, 'tp', axis=1, tiled=True)]
    sub x2 -> x0, matrix products: 135 us -> none  [causal_attention(): jax.nn.softmax(jnp.where(causal, scores, -1e+30), axis=-1)]
    unnamed x6 -> x0, matrix products: 70.2 us -> none
    squeeze x0 -> x6, local copies, waits for them, and re-layouts: none -> 15.5 us  [the longest x1 6.21 us: local_program(): w_down[layer]]
    concatenate x2 -> x6, other arithmetic: 0.51 us -> 12.1 us  [the longest x2 7.1 us: local_program(): jnp.concatenate([pad_in(w_q[layer]), pad_in(w_k[layer]), pad_in(w_v[layer...]
  transfers between devices with their start and end apart: 4 -> 0, of which waited for: 4 -> 0; matrix products, arithmetic and copies ran while one was open for 2% -> 0% of each run, Pallas kernels for 0% -> 0%
where the time goes in v1:
time: 581 us; the launch traced here: 574 us
  Pallas kernels  513 us (88%)
  local copies, waits for them, and re-layouts  34.9 us (6%)
  other arithmetic  24.7 us (4%)
    pallas_call x2, Pallas kernels, attend_scatter(): pl.pallas_call(functools.partial(scatter_kernel, last, head_dim), out_sha...  272 us
    pallas_call x2, Pallas kernels, gather_project(): pl.pallas_call(gather_kernel, out_shape=(qkv_shape, qkv_shape, qkv_shape,...  241 us

profile of v1, /device:TPU:0, one launch (start us, length us, event | category | flops | bytes accessed | tf_op | source)
XLA Modules:
  0.0 573.8 jit_solution(4872992160725185379)
XLA Ops:
  0.0 0.7 slice_bitcast_fusion.12
  0.7 0.6 compare_reduce_fusion
  2.0 0.1 scatter.6
  2.1 0.7 slice_bitcast_fusion.13
  2.8 0.7 slice_bitcast_fusion.14
  3.5 0.6 pad_maximum_fusion.2.b_qkv
  4.1 0.1 iota_bitcast_fusion
  4.1 0.1 add_convert_fusion
  4.3 7.5 %fusion.6 = (f32[8,2,256,16]{3,2,1,0:T(8,128)S(1)}, f32[8,2,256,16]{3,2,1,0:T(8,128)S(1)}, f32[8,2,256,16]{3,2,1,0:T(8,128)S(1)}) fusion(f32[16]{0:T(128)S(1)} %negate_power_fusion, f32[8,2,256]{2,1,0:T(2,128)S(1)} %copy.25), kind=kLoop, calls=%fused_computation.26 | loop fusion | flops 131072 | bytes 802880 | tf_op jit(solution)/shard_map/neg | solution.py:356
  11.8 0.1 pad.83.clone
  11.8 1.9 maximum_maximum_fusion.1.sin_t
  13.7 0.1 pad.86.clone
  13.8 1.9 maximum_maximum_fusion.cos_t
  15.7 0.0 copy-done.6
  15.7 0.0 copy-done.7
  15.7 0.1 fusion.7
  15.8 0.0 copy-done
  15.8 0.3 convert_reduce_fusion
  16.1 0.5 fusion.2
  16.6 1.6 fusion.5.h_hbm
  18.2 0.0 copy-done.4
  18.2 0.1 slice_bitcast_fusion.7
  18.3 0.1 pad.59
  18.4 1.5 copy.30
  19.9 2.4 slice_bitcast_fusion.6
  22.3 0.1 pad.60
  22.4 1.4 copy.31
  23.9 2.4 slice_bitcast_fusion.5
  26.3 1.1 pad.61
  27.4 2.5 copy.32
  29.9 3.8 pad_maximum_fusion.w_qkv
  33.7 0.0 slice-done
  33.7 1.0 slice-done.1
  34.7 3.3 slice_bitcast_fusion.1
  38.0 0.0 copy-done.10
  38.0 0.6 slice_convert_fusion.8
  38.6 121.5 %gather_project_0.1 = (bf16[8,2,256,256]{3,2,1,0:T(8,128)(2,1)}, bf16[8,2,256,256]{3,2,1,0:T(8,128)(2,1)}, bf16[8,2,256,256]{3,2,1,0:T(8,128)(2,1)}, bf16[8,2,256,640]{3,2,1,0:T(8,128)(2,1)}) custom-call(bf16[256,2560]{1,0:T(8,128)(2,1)} %fusion.5.h_hbm, bf16[2560,768]{1,0:T(8,128)(2,1)} %pad_maximum_fusion.w_qkv, bf16[2560,640]{1,0:T(8,128)(2,1)} %get-tuple-element.52.w_up, ...), custom_call_target="tpu_custom_call" | custom-call | tf_op jit(solution)/shard_map/gather_project_0/pallas_call | solution.py:162
  160.1 0.6 slice_convert_fusion.6
  160.7 0.0 copy-done.8
  160.7 0.0 copy-done.9
  160.7 0.6 slice_convert_fusion
  161.4 6.2 %slice_bitcast_fusion = (bf16[640,2560]{1,0:T(8,128)(2,1)}, bf16[640,2560]{1,0:T(8,128)(2,1)}) fusion(bf16[2,640,2560]{2,1,0:T(8,128)(2,1)} %param.32), kind=kLoop, calls=%fused_computation.2 | loop fusion | bytes 13107200 | tf_op jit(solution)/shard_map/squeeze | solution.py:392
  167.6 0.0 copy-done.5
  167.6 1.0 slice_bitcast_fusion.4
  168.6 1.1 pad.66
  169.7 136.2 %attend_scatter_1.1 = (bf16[256,2560]{1,0:T(8,128)(2,1)}, bf16[256,2560]{1,0:T(8,128)(2,1)}) custom-call(bf16[8,2,256,256]{3,2,1,0:T(8,128)(2,1)} %get-tuple-element.39.q_ref, bf16[8,2,256,256]{3,2,1,0:T(8,128)(2,1)} %get-tuple-element.40.k_ref, bf16[8,2,256,256]{3,2,1,0:T(8,128)(2,1)} %get-tuple-element.41.v_ref, ...), custom_call_target="tpu_custom_call" | custom-call | tf_op jit(solution)/shard_map/attend_scatter_1/pallas_call | solution.py:324
  306.0 0.3 scatter.9
  306.3 0.6 pad_maximum_fusion.3.b_qkv
  306.9 0.1 pad.67
  307.0 0.0 copy-start.1
  307.0 0.6 copy.33
  307.6 0.5 copy-done.1
  308.1 0.1 pad.68
  308.2 0.0 copy-start.2
  308.2 1.5 copy.34
  309.7 0.0 copy-done.2
  309.7 0.1 pad.69
  309.8 1.4 copy.35
  311.2 3.3 pad_maximum_fusion.1.w_qkv
  314.6 119.3 %gather_project_2.1 = (bf16[8,2,256,256]{3,2,1,0:T(8,128)(2,1)}, bf16[8,2,256,256]{3,2,1,0:T(8,128)(2,1)}, bf16[8,2,256,256]{3,2,1,0:T(8,128)(2,1)}, bf16[8,2,256,640]{3,2,1,0:T(8,128)(2,1)}) custom-call(bf16[256,2560]{1,0:T(8,128)(2,1)} %get-tuple-element.43.h_hbm, bf16[2560,768]{1,0:T(8,128)(2,1)} %pad_maximum_fusion.1.w_qkv, ...), custom_call_target="tpu_custom_call" | custom-call | tf_op jit(solution)/shard_map/gather_project_2/pallas_call | solution.py:162
  433.9 0.0 copy-done.3
  433.9 1.1 pad.74
  435.0 135.9 %attend_scatter_3.1 = bf16[256,2560]{1,0:T(8,128)(2,1)} custom-call(bf16[8,2,256,256]{3,2,1,0:T(8,128)(2,1)} %get-tuple-element.44.q_ref, bf16[8,2,256,256]{3,2,1,0:T(8,128)(2,1)} %get-tuple-element.45.k_ref, bf16[8,2,256,256]{3,2,1,0:T(8,128)(2,1)} %get-tuple-element.46.v_ref, bf16[8,2,256,640]{3,2,1,0:T(8,128)(2,1)} %get-tuple-element.47.m_ref, ...), custom_call_target="tpu_custom_call" | custom-call | tf_op jit(solution)/shard_map/attend_scatter_3/pallas_call | solution.py:324
  570.9 2.5 copy.39
  (25 shorter events, 0.1 us)
Async XLA Ops:
  13.8 1.9 copy-start.6
  13.8 1.9 copy-start.7
  13.8 2.0 copy-start
  16.1 2.2 copy-start.4
  26.3 7.4 %slice-start = ((s8[6553600]{0:T(1024)(128)(4,1)}), s8[2359296]{0:T(1024)(128)(4,1)S(1)}, s32[]{:S(2)}) async-start(s8[6553600]{0:T(1024)(128)(4,1)} %bitcast.60), calls=%async_computation | async-start | bytes 4718592
  29.9 4.8 slice-start.1
  34.7 3.3 copy-start.10
  38.6 122.1 %copy-start.8 = (bf16[2,2560]{1,0:T(2,128)(2,1)S(1)}, bf16[2,2560]{1,0:T(2,128)(2,1)}, u32[]{:S(2)}) copy-start(bf16[2,2560]{1,0:T(2,128)(2,1)} %param.33) | copy-start | bytes 30724
  38.6 122.1 %copy-start.9 = (bf16[2,2560]{1,0:T(2,128)(2,1)S(1)}, bf16[2,2560]{1,0:T(2,128)(2,1)}, u32[]{:S(2)}) copy-start(bf16[2,2560]{1,0:T(2,128)(2,1)} %param.29) | copy-start | bytes 30724
  161.4 6.2 %copy-start.5 = (bf16[2,2,80,2560]{3,2,1,0:T(8,128)(2,1)S(1)}, bf16[2,2,80,2560]{3,2,1,0:T(8,128)(2,1)}, u32[]{:S(2)}) copy-start(bf16[2,2,80,2560]{3,2,1,0:T(8,128)(2,1)} %param.28) | copy-start | bytes 4915204
  307.0 1.1 copy-start.1
  308.2 1.5 copy-start.2
  314.6 119.3 %copy-start.3 = (bf16[2,80,2560]{2,1,0:T(8,128)(2,1)S(1)}, bf16[2,80,2560]{2,1,0:T(8,128)(2,1)}, u32[]{:S(2)}) copy-start(bf16[2,80,2560]{2,1,0:T(8,128)(2,1)} %get-tuple-element.53) | copy-start | bytes 2457604

commit v2 on v0

v2 whole, which is shorter than its diff:
```python
import functools

import jax
import jax.numpy as jnp
from jax import lax
from jax.experimental import pallas as pl
from jax.experimental.pallas import tpu as pltpu
from jax.sharding import PartitionSpec as P

ROT_DIM = 32
ROPE_BASE = 10000.0
LN_EPS = 1e-5
LANES = 128
RING = 8
LOG2_E = 1.4426950408889634
MESH = pl.DeviceIdType.MESH
VMEM_LIMIT = 67043328
F32 = jnp.float32
BF16 = jnp.bfloat16


def ring_to_chip(pos):
    y = ((pos + 3) // 4) % 2
    z = y * (pos - 1) + (1 - y) * ((RING - pos) % RING)
    return 2 * z + y


def chip_to_ring(chip):
    y = chip % 2
    z = chip // 2
    return y * (z + 1) + (1 - y) * ((RING - z) % RING)


def place():
    me = lax.axis_index("tp")
    core = me % 2
    chip = me // 2
    pos = chip_to_ring(chip)
    right = 2 * ring_to_chip((pos + 1) % RING) + core
    left = 2 * ring_to_chip((pos + RING - 1) % RING) + core
    partner = 2 * chip + (1 - core)
    return core, chip, pos, right, left, partner


def meet(right, left, partner):
    barrier = pltpu.get_barrier_semaphore()
    for other in (right, left, partner):
        pl.semaphore_signal(barrier, inc=1, device_id={"tp": other}, device_id_type=MESH)
    pl.semaphore_wait(barrier, 3)


def layer_norm(hidden, gain, bias):
    x_f32 = hidden.astype(F32)
    mean = jnp.mean(x_f32, axis=-1, keepdims=True)
    centered = x_f32 - mean
    variance = jnp.mean(centered * centered, axis=-1, keepdims=True)
    return (centered * lax.rsqrt(variance + LN_EPS) * gain + bias).astype(BF16)


def layers_kernel(x_ref, wq_hbm, wk_hbm, wv_hbm, wo_hbm, wup_hbm, wdown_hbm, b_qkv, b_up, b_sum, gain, bias,
                  base_cos, base_sin, step_cos, step_sin, out_ref,
                  hbuf, q_all, k_all, v_all, m_all, staged, w_qkv, w_up, w_o, w_down, given, own, acc, top,
                  weight_sem, gather_send, gather_recv, share_send, share_recv,
                  scatter_send, scatter_recv, pair_send, pair_recv, ready):
    layers, heads, head_dim, depth = wq_hbm.shape
    rows = x_ref.shape[0]
    half = rows // 2
    piece = half // 2
    width = heads * LANES
    tile = next(t for t in (512, 256, 128) if depth % t == 0)
    scale = head_dim ** -0.5 * LOG2_E
    core, chip, pos, right, left, partner = place()
    mine, other = pl.ds(pl.multiple_of(core * half, half), half), pl.ds(pl.multiple_of((1 - core) * half, half), half)

    def span_of(part):
        return pl.ds(pl.multiple_of(part * piece, piece), piece)

    def remote(src, dst, send_sem, recv_sem, to):
        return pltpu.make_async_remote_copy(src_ref=src, dst_ref=dst, send_sem=send_sem, recv_sem=recv_sem,
                                            device_id={"tp": to}, device_id_type=MESH)

    def next_of(way):
        return right if way == 0 else left

    def in_copies(layer):
        copies = [pltpu.make_async_copy(hbm.at[layer, head], staged.at[which * heads + head, pl.ds(0, head_dim)],
                                        weight_sem.at[which * heads + head])
                  for which, hbm in enumerate((wq_hbm, wk_hbm, wv_hbm)) for head in range(heads)]
        return copies + [pltpu.make_async_copy(wup_hbm.at[layer], w_up, weight_sem.at[3 * heads])]

    def out_copies(layer):
        copies = [pltpu.make_async_copy(wo_hbm.at[layer, head], w_o.at[pl.ds(head * LANES, head_dim)],
                                        weight_sem.at[3 * heads + 1 + head]) for head in range(heads)]
        return copies + [pltpu.make_async_copy(wdown_hbm.at[layer], w_down, weight_sem.at[4 * heads + 1])]

    def gathered_block(way, step):
        return ring_to_chip((pos + (1 - way) * (RING - step) + way * step) % RING)

    def gather_copy(way, step, sem_step, part):
        ref = hbuf.at[way, gathered_block(way, step), pl.ds(pl.multiple_of(core * half + part * piece, piece), piece)]
        return remote(ref, ref, gather_send.at[way, sem_step, part], gather_recv.at[way, sem_step, part], next_of(way))

    def share_copy(way, step, part, side):
        ref = hbuf.at[way, gathered_block(way, step), pl.ds(pl.multiple_of(side * half + part * piece, piece), piece)]
        return remote(ref, ref, share_send.at[way, step, part], share_recv.at[way, step, part], partner)

    def rotate(value, cosine, sine):
        lane = lax.broadcasted_iota(jnp.int32, value.shape, 1)
        swapped = jnp.where(lane < ROT_DIM // 2, pltpu.roll(value, LANES - ROT_DIM // 2, 1), pltpu.roll(value, ROT_DIM // 2, 1))
        return value * cosine + swapped * sine

    def project(layer, way, step):
        for part in range(2):
            share_copy(way, step, part, 1 - core).wait_recv()
        at = gathered_block(way, step)
        normed = hbuf[way, at]
        cos_0, sin_0, cos_1, sin_1 = base_cos[at], base_sin[at], step_cos[way], step_sin[way]
        lane = lax.broadcasted_iota(jnp.int32, (1, LANES), 1)
        sign = jnp.where(lane < ROT_DIM // 2, -1.0, 1.0)
        cosine = cos_0 * cos_1 - sin_0 * sin_1
        sine = (sin_0 * cos_1 + cos_0 * sin_1) * sign
        for which, out in enumerate((q_all, k_all, v_all)):
            cols = slice(which * width, (which + 1) * width)
            proj = jnp.dot(normed, w_qkv[:, cols], preferred_element_type=F32) + b_qkv[layer, :, cols]
            if which < 2:
                for head in range(heads):
                    lanes = slice(head * LANES, (head + 1) * LANES)
                    out[at, way, :, lanes] = rotate(proj[:, lanes], cosine, sine).astype(BF16)
            else:
                out[at, way] = proj.astype(BF16)
        up = jnp.dot(normed, w_up[...], preferred_element_type=F32) + b_up[layer]
        m_all[at, way] = jax.nn.gelu(up, approximate=True).astype(BF16)

    def scattered_block(way, step):
        return ring_to_chip((pos + (1 - way) * (2 * RING - 1 - step) + way * (1 + step)) % RING)

    def scatter_copy(way, step, part):
        span = span_of(part)
        return remote(hbuf.at[way, step, span], hbuf.at[way, step + 1, span],
                      scatter_send.at[way, step, part], scatter_recv.at[way, step, part], next_of(way))

    def pair_copy(way, step):
        return remote(given.at[way, step % 2], hbuf.at[way, step, pl.ds(half, half)],
                      pair_send.at[way, step], pair_recv.at[way, step], partner)

    def attend(way, at):
        row = lax.broadcasted_iota(jnp.int32, (rows, 1), 0)
        row_side = (row // half + core) % 2
        row_pos = row_side * (2 * half) + way * half + row % half
        col = lax.broadcasted_iota(jnp.int32, (1, 2 * rows), 1)
        col_pos = ((col // half) % 2) * (2 * half) + (col // rows) * half + col % half
        queries = []
        for head in range(heads):
            lanes = slice(head * LANES, (head + 1) * LANES)
            queries.append(jnp.concatenate([q_all[at, way, mine, lanes], q_all[at, way, other, lanes]], axis=0))
            keys = k_all[at, :, :, lanes].reshape(2 * rows, LANES)
            values = v_all[at, :, :, lanes].reshape(2 * rows, LANES)
            score = lax.dot_general(queries[head], keys, (((1,), (1,)), ((), ())), preferred_element_type=F32) * scale
            score = jnp.where(row_pos >= col_pos, score, -1e30)
            peak = jnp.max(score, axis=1, keepdims=True)
            prob = jnp.exp2(score - peak).astype(BF16)
            acc[head] = jnp.dot(prob, values, preferred_element_type=F32)
            top[head] = jnp.broadcast_to(peak, (rows, LANES))

        def body(earlier, carry):
            for head in range(heads):
                lanes = slice(head * LANES, (head + 1) * LANES)
                keys = k_all[earlier, :, :, lanes].reshape(2 * rows, LANES)
                values = v_all[earlier, :, :, lanes].reshape(2 * rows, LANES)
                score = lax.dot_general(queries[head], keys, (((1,), (1,)), ((), ())), preferred_element_type=F32) * scale
                before = top[head][:, :1]
                peak = jnp.maximum(before, jnp.max(score, axis=1, keepdims=True))
                prob = jnp.exp2(score - peak).astype(BF16)
                acc[head] = acc[head] * jnp.exp2(before - peak) + jnp.dot(prob, values, preferred_element_type=F32)
                top[head] = jnp.broadcast_to(peak, (rows, LANES))
            return carry

        lax.fori_loop(0, at, body, 0)
        done = [(acc[head] / acc[head][:, head_dim:head_dim + 1]).astype(BF16) for head in range(heads)]
        return jnp.concatenate(done, axis=1)

    def contribute(way, step, before_send):
        at = scattered_block(way, step)
        attended = attend(way, at)
        up = jnp.concatenate([m_all[at, way, mine], m_all[at, way, other]], axis=0)

        @pl.when(step >= 2)
        def _():
            pair_copy(way, step - 2).wait_send()

        for low in range(0, depth, tile):
            cols = slice(low, low + tile)
            part_sum = (jnp.dot(attended, w_o[:, cols], preferred_element_type=F32)
                        + jnp.dot(up, w_down[:, cols], preferred_element_type=F32))
            own[way, step % 2, :, cols] = part_sum[:half]
            given[way, step % 2, :, cols] = part_sum[half:].astype(BF16)
        before_send()
        pair_copy(way, step).start()

    def total(way, step, part):
        span = span_of(part)
        taken = pl.ds(pl.multiple_of(half + part * piece, piece), piece)
        return own[way, step % 2, span] + hbuf[way, step, taken].astype(F32) + hbuf[way, step, span].astype(F32)

    def tell(phase):
        for to in (right, left, partner):
            pl.semaphore_signal(ready.at[phase], inc=1, device_id={"tp": to}, device_id_type=MESH)

    for copy in in_copies(0):
        copy.start()
    for g in range(3 * heads):
        staged[g, head_dim:] = jnp.zeros((LANES - head_dim, depth), BF16)
    for head in range(heads):
        w_o[head * LANES + head_dim:(head + 1) * LANES] = jnp.zeros((LANES - head_dim, depth), BF16)
    out_ref[...] = x_ref[...]
    meet(right, left, partner)

    def layer_body(layer, carry):
        for copy in out_copies(layer):
            copy.start()
        for way in range(2):
            for part in range(2):
                low = way * half + part * piece
                hbuf[way, chip, pl.ds(pl.multiple_of(core * half + part * piece, piece), piece)] = layer_norm(
                    out_ref[low:low + piece], gain[layer], bias[layer])

        @pl.when(layer > 0)
        def _():
            pl.semaphore_wait(ready.at[2 * layer - 1], 3)

        for part in range(2):
            for way in range(2):
                gather_copy(way, 0, 0, part).start()
                share_copy(way, 0, part, core).start()

        for copy in in_copies(layer):
            copy.wait()
        for g in range(3 * heads):
            w_qkv[:, g * LANES:(g + 1) * LANES] = staged[g].T

        def arrive(event):
            step, part = 1 + event // 2, event % 2
            for way in range(2):
                gather_copy(way, step, step - 1, part).wait_recv()

                @pl.when(step < RING - 1)
                def _():
                    gather_copy(way, step, step, part).start()

                share_copy(way, step, part, core).start()

        def first_units(unit, carry):
            project(layer, unit, 0)
            return carry

        def events(event, carry):
            arrive(event)
            project(layer, (event + 1) % 2, (event + 1) // 2)
            return carry

        lax.fori_loop(0, 2, first_units, 0)
        arrive(0)
        lax.fori_loop(1, 2 * RING - 2, events, 0)
        project(layer, 1, RING - 1)

        def drain_gather(step, carry):
            for way in range(2):
                for part in range(2):
                    @pl.when(step < RING - 1)
                    def _():
                        gather_copy(way, step, step, part).wait_send()

                    share_copy(way, step, part, core).wait_send()
            return carry

        lax.fori_loop(0, RING, drain_gather, 0)
        tell(2 * layer)

        @pl.when(layer < layers - 1)
        def _():
            for copy in in_copies(layer + 1):
                copy.start()

        for copy in out_copies(layer):
            copy.wait()
        for way in range(2):
            hbuf[way, 0, :half] = jnp.zeros((half, depth), BF16)

        def first_parts(way, carry):
            def before_send():
                @pl.when(way == 0)
                def _():
                    pl.semaphore_wait(ready.at[2 * layer], 3)

            contribute(way, 0, before_send)
            return carry

        def scatter_events(event, carry):
            step, part = event // 2, event % 2
            for way in range(2):
                @pl.when(part == 0)
                def _():
                    pair_copy(way, step).wait_recv()

                @pl.when(step > 0)
                def _():
                    scatter_copy(way, step - 1, part).wait_recv()

                hbuf[way, step, span_of(part)] = total(way, step, part).astype(BF16)
                scatter_copy(way, step, part).start()
            contribute(part, step + 1, lambda: None)
            return carry

        lax.fori_loop(0, 2, first_parts, 0)
        lax.fori_loop(0, 2 * RING - 2, scatter_events, 0)
        for part in range(2):
            for way in range(2):
                if part == 0:
                    pair_copy(way, RING - 1).wait_recv()
                scatter_copy(way, RING - 2, part).wait_recv()
                low = way * half + part * piece
                hidden = out_ref[low:low + piece].astype(F32) + total(way, RING - 1, part) + b_sum[layer]
                out_ref[low:low + piece] = hidden.astype(BF16)

        def drain_scatter(step, carry):
            for way in range(2):
                for part in range(2):
                    scatter_copy(way, step, part).wait_send()
            return carry

        lax.fori_loop(0, RING - 1, drain_scatter, 0)
        for way in range(2):
            for step in (RING - 2, RING - 1):
                pair_copy(way, step).wait_send()

        @pl.when(layer < layers - 1)
        def _():
            tell(2 * layer + 1)

        return carry

    lax.fori_loop(0, layers, layer_body, 0)


def run_layers(x, w_q, w_k, w_v, w_o, w_up, w_down, b_qkv, b_up, b_sum, gain, bias, tables):
    rows, depth = x.shape
    layers, heads, head_dim, _ = w_q.shape
    width, hidden_width = heads * LANES, w_up.shape[2]
    half = rows // 2
    vmem = pl.BlockSpec(memory_space=pltpu.VMEM)
    hbm = pl.BlockSpec(memory_space=pl.ANY)
    return pl.pallas_call(
        layers_kernel,
        out_shape=jax.ShapeDtypeStruct((rows, depth), BF16),
        in_specs=[vmem] + [hbm] * 6 + [vmem] * 9,
        out_specs=vmem,
        scratch_shapes=[
            pltpu.VMEM((2, RING, rows, depth), BF16),
            pltpu.VMEM((RING, 2, rows, width), BF16),
            pltpu.VMEM((RING, 2, rows, width), BF16),
            pltpu.VMEM((RING, 2, rows, width), BF16),
            pltpu.VMEM((RING, 2, rows, hidden_width), BF16),
            pltpu.VMEM((3 * heads, LANES, depth), BF16),
            pltpu.VMEM((depth, 3 * width), BF16),
            pltpu.VMEM((depth, hidden_width), BF16),
            pltpu.VMEM((width, depth), BF16),
            pltpu.VMEM((hidden_width, depth), BF16),
            pltpu.VMEM((2, 2, half, depth), BF16),
            pltpu.VMEM((2, 2, half, depth), F32),
            pltpu.VMEM((heads, rows, LANES), F32),
            pltpu.VMEM((heads, rows, LANES), F32),
            pltpu.SemaphoreType.DMA((4 * heads + 2,)),
            pltpu.SemaphoreType.DMA((2, RING, 2)),
            pltpu.SemaphoreType.DMA((2, RING, 2)),
            pltpu.SemaphoreType.DMA((2, RING, 2)),
            pltpu.SemaphoreType.DMA((2, RING, 2)),
            pltpu.SemaphoreType.DMA((2, RING, 2)),
            pltpu.SemaphoreType.DMA((2, RING, 2)),
            pltpu.SemaphoreType.DMA((2, RING)),
            pltpu.SemaphoreType.DMA((2, RING)),
            pltpu.SemaphoreType.REGULAR((2 * layers,)),
        ],
        compiler_params=pltpu.CompilerParams(collective_id=0, has_side_effects=True, vmem_limit_bytes=VMEM_LIMIT),
        name="layers",
    )(x, w_q, w_k, w_v, w_o, w_up, w_down, b_qkv, b_up, b_sum, gain, bias, *tables)


def rotary_tables(rows):
    half = rows // 2
    way, core, row = jnp.meshgrid(jnp.arange(2), jnp.arange(2), jnp.arange(half), indexing="ij")
    offset = (core * rows + way * half + row).astype(F32).reshape(2, rows, 1)
    base = (jnp.arange(RING, dtype=F32) * (2 * rows)).reshape(RING, 1, 1)
    lane = jnp.arange(LANES)
    pair = (lane % (ROT_DIM // 2)).astype(F32)
    inv_freq = jnp.where(lane < ROT_DIM, 1.0 / (ROPE_BASE ** (pair * (2.0 / ROT_DIM))), 0.0)
    return jnp.cos(base * inv_freq), jnp.sin(base * inv_freq), jnp.cos(offset * inv_freq), jnp.sin(offset * inv_freq)


def solution(mesh):
    head_spec = P(None, None, "tp", None)
    head_bias_spec = P(None, "tp", None)
    in_specs = (P("dp", "tp", None), P(), P(), head_spec, head_bias_spec, head_spec, head_bias_spec, head_spec, head_bias_spec,
                P(None, "tp", None, None), P(), P(None, None, "tp"), P(None, "tp"), P(None, "tp", None), P())

    def local_program(x_loc, ln_gain, ln_bias, w_q, b_q, w_k, b_k, w_v, b_v, w_o, b_o, w_up, b_up, w_down, b_down):
        layers, _, heads, head_dim = w_q.shape
        spare = LANES - head_dim

        def heads_first(weight):
            return jnp.transpose(weight, (0, 2, 3, 1))

        def wide_bias(vector, fill):
            lane = jnp.arange(LANES)
            padded = jnp.pad(vector.astype(F32), ((0, 0), (0, 0), (0, spare)))
            return jnp.where(lane == head_dim, fill, padded).reshape(layers, 1, heads * LANES)

        def row(vector):
            return vector.astype(F32).reshape(layers, 1, -1)

        b_qkv = jnp.concatenate([wide_bias(b_q, 0.0), wide_bias(b_k, 0.0), wide_bias(b_v, 1.0)], axis=2)
        out = run_layers(x_loc[0], heads_first(w_q), heads_first(w_k), heads_first(w_v), w_o, w_up, w_down, b_qkv, row(b_up),
                         row(b_o) + row(b_down), row(ln_gain), row(ln_bias), rotary_tables(x_loc.shape[1]))
        return out[None]

    return jax.shard_map(local_program, mesh=mesh, in_specs=in_specs, out_specs=P("dp", "tp", None), check_vma=False)
```

time: 1090 us -> 487 us (0.45)
  waiting for transfers between devices: 615 us -> 0 us
  Pallas kernels: 0 us -> 475 us
  matrix products: 417 us -> 0 us
  other arithmetic: 30.3 us -> 4.66 us
  between operations: 14.1 us -> 0.04 us
    pallas_call x0 -> x1, Pallas kernels: none -> 475 us  [run_layers(): pl.pallas_call(layers_kernel, out_shape=jax.ShapeDtypeStruct((rows, depth...]
    reduce_scatter x2 -> x0, waiting for transfers between devices: 415 us -> none  [local_program(): returned = lax.psum_scatter(part_sum, 'tp', scatter_dimension=1, tiled=True)]
    dot_general x8 -> x0, matrix products: 212 us -> none  [the longest x2 86.2 us: causal_attention(): jnp.einsum('bhqk,bhke->bhqe', attn_probs, values, preferred_element_type=...]
    all_gather x2 -> x0, waiting for transfers between devices: 200 us -> none  [local_program(): gathered = lax.all_gather(normed, 'tp', axis=1, tiled=True)]
    sub x2 -> x0, matrix products: 135 us -> none  [causal_attention(): jax.nn.softmax(jnp.where(causal, scores, -1e+30), axis=-1)]
    unnamed x6 -> x0, matrix products: 70.2 us -> none
    ge x1 -> x0, other arithmetic: 11.5 us -> none  [causal_attention(): causal = jnp.arange(seq_len)[:, None] >= jnp.arange(seq_len)[None, :]]
  transfers between devices with their start and end apart: 4 -> 0, of which waited for: 4 -> 0; matrix products, arithmetic and copies ran while one was open for 2% -> 0% of each run, Pallas kernels for 0% -> 0%
where the time goes in v2:
time: 487 us
  Pallas kernels  475 us (98%)
  local copies, waits for them, and re-layouts  7.11 us (1%)
    pallas_call x1, Pallas kernels, run_layers(): pl.pallas_call(layers_kernel, out_shape=jax.ShapeDtypeStruct((rows, depth...  475 us

profile of v2, /device:TPU:0, one launch (start us, length us, event | category | flops | bytes accessed | tf_op | source)
XLA Modules:
  0.0 486.6 jit_solution(6662040739268207734)
XLA Ops:
  0.0 0.1 iota_bitcast_fusion
  0.1 0.1 add_convert_fusion
  0.2 0.1 mul.107
  0.3 0.7 multiply_sine_fusion.1
  1.0 1.3 reshape.156.b_up
  2.3 0.7 convert_select_fusion.2
  3.0 0.6 pad_maximum_fusion.b_qkv
  3.6 1.3 reshape.158.gain
  4.9 1.3 reshape.160.bias
  6.2 0.7 convert_add_fusion
  6.9 0.6 add.45.b_sum
  7.6 1.8 multiply_sine_fusion
  9.3 474.8 %layers.1 = bf16[256,2560]{1,0:T(8,128)(2,1)} custom-call(bf16[256,2560]{1,0:T(8,128)(2,1)} %bitcast.17, bf16[2,2,80,2560]{3,2,1,0:T(8,128)(2,1)} %bitcast.14, bf16[2,2,80,2560]{3,2,1,0:T(8,128)(2,1)} %bitcast.15, bf16[2,2,80,2560]{3,2,1,0:T(8,128)(2,1)} %bitcast.16, bf16[2,2,80,2560]{3,2,1,0:T(8,128)(2,1)} %wo_hbm.1, bf16[2,2560,640]{2,1,0:T(8,128)(2,1)} %wup_hbm.1, ...), custom_call_target="tpu_custom_call" | custom-call | tf_op jit(solution)/shard_map/layers/pallas_call | solution.py:352
  484.1 2.5 copy.18
  (5 shorter events, 0.0 us)

commit v3 on v2

--- a/solution.py
+++ b/solution.py
@@ -57,9 +57,9 @@
     return (centered * lax.rsqrt(variance + LN_EPS) * gain + bias).astype(BF16)
 
 
-def layers_kernel(x_ref, wq_hbm, wk_hbm, wv_hbm, wo_hbm, wup_hbm, wdown_hbm, b_qkv, b_up, b_sum, gain, bias,
-                  base_cos, base_sin, step_cos, step_sin, out_ref,
-                  hbuf, q_all, k_all, v_all, m_all, staged, w_qkv, w_up, w_o, w_down, given, own, acc, top,
+def layers_kernel(x_ref, wq_hbm, wk_hbm, wv_hbm, wo_hbm, wup_hbm, wdown_hbm, bq_ref, bk_ref, bv_ref, bup_ref, bo_ref, bdown_ref,
+                  gain_ref, bias_ref, base_cos, base_sin, step_cos, step_sin, out_ref,
+                  b_qkv, b_up, b_sum, gain, bias, hbuf, q_all, k_all, v_all, m_all, staged, w_qkv, w_up, w_o, w_down, given, own, acc, top,
                   weight_sem, gather_send, gather_recv, share_send, share_recv,
                   scatter_send, scatter_recv, pair_send, pair_recv, ready):
     layers, heads, head_dim, depth = wq_hbm.shape
@@ -125,9 +125,15 @@
             if which < 2:
                 for head in range(heads):
                     lanes = slice(head * LANES, (head + 1) * LANES)
-                    out[at, way, :, lanes] = rotate(proj[:, lanes], cosine, sine).astype(BF16)
+                    turned = rotate(proj[:, lanes], cosine, sine)
+                    if which == 0:
+                        out[at, way, lanes] = turned.T.astype(BF16)
+                    else:
+                        out[at, way, :, lanes] = turned.astype(BF16)
             else:
-                out[at, way] = proj.astype(BF16)
+                for head in range(heads):
+                    lanes = slice(head * LANES, (head + 1) * LANES)
+                    out[at, way, lanes] = proj[:, lanes].T.astype(BF16)
         up = jnp.dot(normed, w_up[...], preferred_element_type=F32) + b_up[layer]
         m_all[at, way] = jax.nn.gelu(up, approximate=True).astype(BF16)
 
@@ -143,45 +149,70 @@
         return remote(given.at[way, step % 2], hbuf.at[way, step, pl.ds(half, half)],
                       pair_send.at[way, step], pair_recv.at[way, step], partner)
 
-    def attend(way, at):
-        row = lax.broadcasted_iota(jnp.int32, (rows, 1), 0)
-        row_side = (row // half + core) % 2
-        row_pos = row_side * (2 * half) + way * half + row % half
-        col = lax.broadcasted_iota(jnp.int32, (1, 2 * rows), 1)
-        col_pos = ((col // half) % 2) * (2 * half) + (col // rows) * half + col % half
-        queries = []
+    def fresh(way, slot):
+        acc[way, slot] = jnp.zeros((heads, LANES, rows), F32)
+        top[way, slot] = jnp.full((heads, 1, rows), -1e30, F32)
+
+    def attend(way, slot, at, block, diagonal):
+        if diagonal:
+            key = lax.broadcasted_iota(jnp.int32, (2 * rows, 1), 0)
+            key_pos = ((key // half) % 2) * (2 * half) + (key // rows) * half + key % half
+            query = lax.broadcasted_iota(jnp.int32, (1, rows), 1)
+            query_pos = ((query // half + core) % 2) * (2 * half) + way * half + query % half
+            seen = query_pos >= key_pos
         for head in range(heads):
             lanes = slice(head * LANES, (head + 1) * LANES)
-            queries.append(jnp.concatenate([q_all[at, way, mine, lanes], q_all[at, way, other, lanes]], axis=0))
-            keys = k_all[at, :, :, lanes].reshape(2 * rows, LANES)
-            values = v_all[at, :, :, lanes].reshape(2 * rows, LANES)
-            score = lax.dot_general(queries[head], keys, (((1,), (1,)), ((), ())), preferred_element_type=F32) * scale
-            score = jnp.where(row_pos >= col_pos, score, -1e30)
-            peak = jnp.max(score, axis=1, keepdims=True)
+            queries = jnp.concatenate([q_all[at, way, lanes, mine], q_all[at, way, lanes, other]], axis=1)
+            keys = k_all[block, :, :, lanes].reshape(2 * rows, LANES)
+            score = jnp.dot(keys, queries, preferred_element_type=F32) * scale
+            if diagonal:
+                score = jnp.where(seen, score, -1e30)
+            before = top[way, slot, head]
+            peak = jnp.maximum(before, jnp.max(score, axis=0, keepdims=True))
             prob = jnp.exp2(score - peak).astype(BF16)
-            acc[head] = jnp.dot(prob, values, preferred_element_type=F32)
-            top[head] = jnp.broadcast_to(peak, (rows, LANES))
-
-        def body(earlier, carry):
-            for head in range(heads):
-                lanes = slice(head * LANES, (head + 1) * LANES)
-                keys = k_all[earlier, :, :, lanes].reshape(2 * rows, LANES)
-                values = v_all[earlier, :, :, lanes].reshape(2 * rows, LANES)
-                score = lax.dot_general(queries[head], keys, (((1,), (1,)), ((), ())), preferred_element_type=F32) * scale
-                before = top[head][:, :1]
-                peak = jnp.maximum(before, jnp.max(score, axis=1, keepdims=True))
-                prob = jnp.exp2(score - peak).astype(BF16)
-                acc[head] = acc[head] * jnp.exp2(before - peak) + jnp.dot(prob, values, preferred_element_type=F32)
-                top[head] = jnp.broadcast_to(peak, (rows, LANES))
-            return carry
-
-        lax.fori_loop(0, at, body, 0)
-        done = [(acc[head] / acc[head][:, head_dim:head_dim + 1]).astype(BF16) for head in range(heads)]
+            weighed = (jnp.dot(v_all[block, 0, lanes], prob[:rows], preferred_element_type=F32)
+                       + jnp.dot(v_all[block, 1, lanes], prob[rows:], preferred_element_type=F32))
+            acc[way, slot, head] = acc[way, slot, head] * jnp.exp2(before - peak) + weighed
+            top[way, slot, head] = peak
+
+    def attend_ahead(offset):
+        block = ring_to_chip((pos + offset) % RING)
+
+        def queries_of(unit, carry):
+            way, step = unit % 2, unit // 2
+            at = scattered_block(way, step)
+
+            @pl.when(block < at)
+            def _():
+                attend(way, step, at, block, False)
+
+            return carry
+
+        lax.fori_loop(0, 4, queries_of, 0)
+
+    def attended_by(way, step):
+        at, slot = scattered_block(way, step), step % 2
+
+        @pl.when(step >= 2)
+        def _():
+            fresh(way, slot)
+
+            def body(earlier, carry):
+                attend(way, slot, at, earlier, False)
+                return carry
+
+            lax.fori_loop(0, at, body, 0)
+
+        attend(way, slot, at, at, True)
+        done = []
+        for head in range(heads):
+            sums = acc[way, slot, head]
+            done.append((sums / sums[head_dim:head_dim + 1]).T.astype(BF16))
         return jnp.concatenate(done, axis=1)
 
     def contribute(way, step, before_send):
         at = scattered_block(way, step)
-        attended = attend(way, at)
+        attended = attended_by(way, step)
         up = jnp.concatenate([m_all[at, way, mine], m_all[at, way, other]], axis=0)
 
         @pl.when(step >= 2)
@@ -212,6 +243,21 @@
         staged[g, head_dim:] = jnp.zeros((LANES - head_dim, depth), BF16)
     for head in range(heads):
         w_o[head * LANES + head_dim:(head + 1) * LANES] = jnp.zeros((LANES - head_dim, depth), BF16)
+    for wide, ref in ((b_up, bup_ref), (gain, gain_ref), (bias, bias_ref)):
+        rows_f32 = ref[...].astype(F32)
+        for layer in range(layers):
+            wide[layer] = rows_f32[layer:layer + 1]
+    rows_f32 = bo_ref[...].astype(F32) + bdown_ref[...].astype(F32)
+    for layer in range(layers):
+        b_sum[layer] = rows_f32[layer:layer + 1]
+    column = lax.broadcasted_iota(jnp.int32, (1, 3 * width), 1)
+    for layer in range(layers):
+        b_qkv[layer] = jnp.where((column >= 2 * width) & (column % LANES == head_dim), 1.0, 0.0)
+        for which, ref in enumerate((bq_ref, bk_ref, bv_ref)):
+            heads_f32 = ref[layer].astype(F32)
+            for head in range(heads):
+                low = which * width + head * LANES
+                b_qkv[layer, :, low:low + head_dim] = heads_f32[head:head + 1]
     out_ref[...] = x_ref[...]
     meet(right, left, partner)
 
@@ -256,12 +302,27 @@
         def events(event, carry):
             arrive(event)
             project(layer, (event + 1) % 2, (event + 1) // 2)
-            return carry
+
+            @pl.when(event >= RING)
+            def _():
+                far, odd = (event - RING) // 2, event % 2
+                attend_ahead((1 - odd) * (RING // 2 - far) + odd * (RING // 2 + far) * ((far + 1) // 2))
+
+            return carry
+
+        def nearest(side, carry):
+            attend_ahead(1 + side * (RING - 2))
+            return carry
+
+        for way in range(2):
+            for slot in range(2):
+                fresh(way, slot)
 
         lax.fori_loop(0, 2, first_units, 0)
         arrive(0)
         lax.fori_loop(1, 2 * RING - 2, events, 0)
         project(layer, 1, RING - 1)
+        lax.fori_loop(0, 2, nearest, 0)
 
         def drain_gather(step, carry):
             for way in range(2):
@@ -342,7 +403,7 @@
     lax.fori_loop(0, layers, layer_body, 0)
 
 
-def run_layers(x, w_q, w_k, w_v, w_o, w_up, w_down, b_qkv, b_up, b_sum, gain, bias, tables):
+def run_layers(x, w_q, w_k, w_v, w_o, w_up, w_down, vectors, tables):
     rows, depth = x.shape
     layers, heads, head_dim, _ = w_q.shape
     width, hidden_width = heads * LANES, w_up.shape[2]
@@ -352,13 +413,18 @@
     return pl.pallas_call(
         layers_kernel,
         out_shape=jax.ShapeDtypeStruct((rows, depth), BF16),
-        in_specs=[vmem] + [hbm] * 6 + [vmem] * 9,
+        in_specs=[vmem] + [hbm] * 6 + [vmem] * 12,
         out_specs=vmem,
         scratch_shapes=[
+            pltpu.VMEM((layers, 1, 3 * width), F32),
+            pltpu.VMEM((layers, 1, hidden_width), F32),
+            pltpu.VMEM((layers, 1, depth), F32),
+            pltpu.VMEM((layers, 1, depth), F32),
+            pltpu.VMEM((layers, 1, depth), F32),
             pltpu.VMEM((2, RING, rows, depth), BF16),
+            pltpu.VMEM((RING, 2, width, rows), BF16),
             pltpu.VMEM((RING, 2, rows, width), BF16),
-            pltpu.VMEM((RING, 2, rows, width), BF16),
-            pltpu.VMEM((RING, 2, rows, width), BF16),
+            pltpu.VMEM((RING, 2, width, rows), BF16),
             pltpu.VMEM((RING, 2, rows, hidden_width), BF16),
             pltpu.VMEM((3 * heads, LANES, depth), BF16),
             pltpu.VMEM((depth, 3 * width), BF16),
@@ -367,8 +433,8 @@
             pltpu.VMEM((hidden_width, depth), BF16),
             pltpu.VMEM((2, 2, half, depth), BF16),
             pltpu.VMEM((2, 2, half, depth), F32),
-            pltpu.VMEM((heads, rows, LANES), F32),
-            pltpu.VMEM((heads, rows, LANES), F32),
+            pltpu.VMEM((2, 2, heads, LANES, rows), F32),
+            pltpu.VMEM((2, 2, heads, 1, rows), F32),
             pltpu.SemaphoreType.DMA((4 * heads + 2,)),
             pltpu.SemaphoreType.DMA((2, RING, 2)),
             pltpu.SemaphoreType.DMA((2, RING, 2)),
@@ -382,7 +448,7 @@
         ],
         compiler_params=pltpu.CompilerParams(collective_id=0, has_side_effects=True, vmem_limit_bytes=VMEM_LIMIT),
         name="layers",
-    )(x, w_q, w_k, w_v, w_o, w_up, w_down, b_qkv, b_up, b_sum, gain, bias, *tables)
+    )(x, w_q, w_k, w_v, w_o, w_up, w_down, *vectors, *tables)
 
 
 def rotary_tables(rows):
@@ -403,23 +469,11 @@
                 P(None, "tp", None, None), P(), P(None, None, "tp"), P(None, "tp"), P(None, "tp", None), P())
 
     def local_program(x_loc, ln_gain, ln_bias, w_q, b_q, w_k, b_k, w_v, b_v, w_o, b_o, w_up, b_up, w_down, b_down):
-        layers, _, heads, head_dim = w_q.shape
-        spare = LANES - head_dim
-
         def heads_first(weight):
             return jnp.transpose(weight, (0, 2, 3, 1))
 
-        def wide_bias(vector, fill):
-            lane = jnp.arange(LANES)
-            padded = jnp.pad(vector.astype(F32), ((0, 0), (0, 0), (0, spare)))
-            return jnp.where(lane == head_dim, fill, padded).reshape(layers, 1, heads * LANES)
-
-        def row(vector):
-            return vector.astype(F32).reshape(layers, 1, -1)
-
-        b_qkv = jnp.concatenate([wide_bias(b_q, 0.0), wide_bias(b_k, 0.0), wide_bias(b_v, 1.0)], axis=2)
-        out = run_layers(x_loc[0], heads_first(w_q), heads_first(w_k), heads_first(w_v), w_o, w_up, w_down, b_qkv, row(b_up),
-                         row(b_o) + row(b_down), row(ln_gain), row(ln_bias), rotary_tables(x_loc.shape[1]))
+        out = run_layers(x_loc[0], heads_first(w_q), heads_first(w_k), heads_first(w_v), w_o, w_up, w_down,
+                         (b_q, b_k, b_v, b_up, b_o, b_down, ln_gain, ln_bias), rotary_tables(x_loc.shape[1]))
         return out[None]
 
     return jax.shard_map(local_program, mesh=mesh, in_specs=in_specs, out_specs=P("dp", "tp", None), check_vma=False)

time: 487 us -> 467 us (0.959)
  Pallas kernels: 475 us -> 461 us
    pallas_call x1, Pallas kernels: 475 us -> 461 us  [run_layers(): pl.pallas_call(layers_kernel, out_shape=jax.ShapeDtypeStruct((rows, depth...]
where the time goes in v3:
time: 467 us; the launch traced here: 466 us
  Pallas kernels  461 us (99%)
    pallas_call x1, Pallas kernels, run_layers(): pl.pallas_call(layers_kernel, out_shape=jax.ShapeDtypeStruct((rows, depth...  461 us

profile of v3, /device:TPU:0, one launch (start us, length us, event | category | flops | bytes accessed | tf_op | source)
XLA Modules:
  0.0 466.4 jit_solution(11303508969919702004)
XLA Ops:
  0.0 0.1 iota_bitcast_fusion
  0.1 0.1 add_convert_fusion
  0.2 0.1 mul.107
  0.3 0.7 multiply_sine_fusion.1
  1.0 1.8 multiply_sine_fusion
  2.8 461.2 %layers.1 = bf16[256,2560]{1,0:T(8,128)(2,1)} custom-call(bf16[256,2560]{1,0:T(8,128)(2,1)} %bitcast.14, bf16[2,2,80,2560]{3,2,1,0:T(8,128)(2,1)} %bitcast.11, bf16[2,2,80,2560]{3,2,1,0:T(8,128)(2,1)} %bitcast.12, bf16[2,2,80,2560]{3,2,1,0:T(8,128)(2,1)} %bitcast.13, bf16[2,2,80,2560]{3,2,1,0:T(8,128)(2,1)} %wo_hbm.1, bf16[2,2560,640]{2,1,0:T(8,128)(2,1)} %wup_hbm.1, ...), custom_call_target="tpu_custom_call" | custom-call | tf_op jit(solution)/shard_map/layers/pallas_call | solution.py:413
  464.0 2.5 copy.18
  (4 shorter events, 0.0 us)

commit v4 on v3

--- a/solution.py
+++ b/solution.py
@@ -12,6 +12,7 @@
 LN_EPS = 1e-5
 LANES = 128
 RING = 8
+PARTS = 4
 LOG2_E = 1.4426950408889634
 MESH = pl.DeviceIdType.MESH
 VMEM_LIMIT = 67043328
@@ -65,7 +66,8 @@
     layers, heads, head_dim, depth = wq_hbm.shape
     rows = x_ref.shape[0]
     half = rows // 2
-    piece = half // 2
+    piece = half // PARTS
+    group = PARTS // 2
     width = heads * LANES
     tile = next(t for t in (512, 256, 128) if depth % t == 0)
     scale = head_dim ** -0.5 * LOG2_E
@@ -110,7 +112,7 @@
         return value * cosine + swapped * sine
 
     def project(layer, way, step):
-        for part in range(2):
+        for part in range(PARTS):
             share_copy(way, step, part, 1 - core).wait_recv()
         at = gathered_block(way, step)
         normed = hbuf[way, at]
@@ -265,7 +267,7 @@
         for copy in out_copies(layer):
             copy.start()
         for way in range(2):
-            for part in range(2):
+            for part in range(PARTS):
                 low = way * half + part * piece
                 hbuf[way, chip, pl.ds(pl.multiple_of(core * half + part * piece, piece), piece)] = layer_norm(
                     out_ref[low:low + piece], gain[layer], bias[layer])
@@ -274,7 +276,7 @@
         def _():
             pl.semaphore_wait(ready.at[2 * layer - 1], 3)
 
-        for part in range(2):
+        for part in range(PARTS):
             for way in range(2):
                 gather_copy(way, 0, 0, part).start()
                 share_copy(way, 0, part, core).start()
@@ -285,15 +287,17 @@
             w_qkv[:, g * LANES:(g + 1) * LANES] = staged[g].T
 
         def arrive(event):
-            step, part = 1 + event // 2, event % 2
-            for way in range(2):
-                gather_copy(way, step, step - 1, part).wait_recv()
-
-                @pl.when(step < RING - 1)
-                def _():
-                    gather_copy(way, step, step, part).start()
-
-                share_copy(way, step, part, core).start()
+            step = 1 + event // 2
+            for index in range(group):
+                part = event % 2 * group + index
+                for way in range(2):
+                    gather_copy(way, step, step - 1, part).wait_recv()
+
+                    @pl.when(step < RING - 1)
+                    def _():
+                        gather_copy(way, step, step, part).start()
+
+                    share_copy(way, step, part, core).start()
 
         def first_units(unit, carry):
             project(layer, unit, 0)
@@ -326,7 +330,7 @@
 
         def drain_gather(step, carry):
             for way in range(2):
-                for part in range(2):
+                for part in range(PARTS):
                     @pl.when(step < RING - 1)
                     def _():
                         gather_copy(way, step, step, part).wait_send()
@@ -357,24 +361,27 @@
             return carry
 
         def scatter_events(event, carry):
-            step, part = event // 2, event % 2
-            for way in range(2):
-                @pl.when(part == 0)
-                def _():
-                    pair_copy(way, step).wait_recv()
-
-                @pl.when(step > 0)
-                def _():
-                    scatter_copy(way, step - 1, part).wait_recv()
-
-                hbuf[way, step, span_of(part)] = total(way, step, part).astype(BF16)
-                scatter_copy(way, step, part).start()
-            contribute(part, step + 1, lambda: None)
+            step, second = event // 2, event % 2
+            for index in range(group):
+                part = second * group + index
+                for way in range(2):
+                    if index == 0:
+                        @pl.when(second == 0)
+                        def _():
+                            pair_copy(way, step).wait_recv()
+
+                    @pl.when(step > 0)
+                    def _():
+                        scatter_copy(way, step - 1, part).wait_recv()
+
+                    hbuf[way, step, span_of(part)] = total(way, step, part).astype(BF16)
+                    scatter_copy(way, step, part).start()
+            contribute(second, step + 1, lambda: None)
             return carry
 
         lax.fori_loop(0, 2, first_parts, 0)
         lax.fori_loop(0, 2 * RING - 2, scatter_events, 0)
-        for part in range(2):
+        for part in range(PARTS):
             for way in range(2):
                 if part == 0:
                     pair_copy(way, RING - 1).wait_recv()
@@ -385,7 +392,7 @@
 
         def drain_scatter(step, carry):
             for way in range(2):
-                for part in range(2):
+                for part in range(PARTS):
                     scatter_copy(way, step, part).wait_send()
             return carry
 
@@ -436,12 +443,12 @@
             pltpu.VMEM((2, 2, heads, LANES, rows), F32),
             pltpu.VMEM((2, 2, heads, 1, rows), F32),
             pltpu.SemaphoreType.DMA((4 * heads + 2,)),
-            pltpu.SemaphoreType.DMA((2, RING, 2)),
-            pltpu.SemaphoreType.DMA((2, RING, 2)),
-            pltpu.SemaphoreType.DMA((2, RING, 2)),
-            pltpu.SemaphoreType.DMA((2, RING, 2)),
-            pltpu.SemaphoreType.DMA((2, RING, 2)),
-            pltpu.SemaphoreType.DMA((2, RING, 2)),
+            pltpu.SemaphoreType.DMA((2, RING, PARTS)),
+            pltpu.SemaphoreType.DMA((2, RING, PARTS)),
+            pltpu.SemaphoreType.DMA((2, RING, PARTS)),
+            pltpu.SemaphoreType.DMA((2, RING, PARTS)),
+            pltpu.SemaphoreType.DMA((2, RING, PARTS)),
+            pltpu.SemaphoreType.DMA((2, RING, PARTS)),
             pltpu.SemaphoreType.DMA((2, RING)),
             pltpu.SemaphoreType.DMA((2, RING)),
             pltpu.SemaphoreType.REGULAR((2 * layers,)),

time: 467 us -> 468 us (level)
  no operation moved by 1% of the time
where the time goes in v4:
time: 468 us
  Pallas kernels  462 us (99%)
    pallas_call x1, Pallas kernels, run_layers(): pl.pallas_call(layers_kernel, out_shape=jax.ShapeDtypeStruct((rows, depth...  462 us

profile of v4, /device:TPU:0, one launch (start us, length us, event | category | flops | bytes accessed | tf_op | source)
XLA Modules:
  0.0 467.6 jit_solution(7910813896191572815)
XLA Ops:
  0.0 0.1 iota_bitcast_fusion
  0.1 0.1 add_convert_fusion
  0.2 0.1 mul.107
  0.3 0.7 multiply_sine_fusion.1
  1.0 1.8 multiply_sine_fusion
  2.8 462.3 %layers.1 = bf16[256,2560]{1,0:T(8,128)(2,1)} custom-call(bf16[256,2560]{1,0:T(8,128)(2,1)} %bitcast.14, bf16[2,2,80,2560]{3,2,1,0:T(8,128)(2,1)} %bitcast.11, bf16[2,2,80,2560]{3,2,1,0:T(8,128)(2,1)} %bitcast.12, bf16[2,2,80,2560]{3,2,1,0:T(8,128)(2,1)} %bitcast.13, bf16[2,2,80,2560]{3,2,1,0:T(8,128)(2,1)} %wo_hbm.1, bf16[2,2560,640]{2,1,0:T(8,128)(2,1)} %wup_hbm.1, ...), custom_call_target="tpu_custom_call" | custom-call | tf_op jit(solution)/shard_map/layers/pallas_call | solution.py:420
  465.1 2.5 copy.18
  (4 shorter events, 0.0 us)

commit v5 on v4

--- a/solution.py
+++ b/solution.py
@@ -12,7 +12,7 @@
 LN_EPS = 1e-5
 LANES = 128
 RING = 8
-PARTS = 4
+PARTS = 2
 LOG2_E = 1.4426950408889634
 MESH = pl.DeviceIdType.MESH
 VMEM_LIMIT = 67043328
@@ -43,11 +43,11 @@
     return core, chip, pos, right, left, partner
 
 
-def meet(right, left, partner):
+def call(right, left, partner):
     barrier = pltpu.get_barrier_semaphore()
     for other in (right, left, partner):
         pl.semaphore_signal(barrier, inc=1, device_id={"tp": other}, device_id_type=MESH)
-    pl.semaphore_wait(barrier, 3)
+    return barrier
 
 
 def layer_norm(hidden, gain, bias):
@@ -98,12 +98,15 @@
     def gathered_block(way, step):
         return ring_to_chip((pos + (1 - way) * (RING - step) + way * step) % RING)
 
-    def gather_copy(way, step, sem_step, part):
-        ref = hbuf.at[way, gathered_block(way, step), pl.ds(pl.multiple_of(core * half + part * piece, piece), piece)]
-        return remote(ref, ref, gather_send.at[way, sem_step, part], gather_recv.at[way, sem_step, part], next_of(way))
+    def gather_rows(way, step, part, side):
+        return hbuf.at[way, step, pl.ds(pl.multiple_of(side * half + part * piece, piece), piece)]
+
+    def gather_copy(way, step, part):
+        return remote(gather_rows(way, step, part, core), gather_rows(way, step + 1, part, core),
+                      gather_send.at[way, step, part], gather_recv.at[way, step, part], next_of(way))
 
     def share_copy(way, step, part, side):
-        ref = hbuf.at[way, gathered_block(way, step), pl.ds(pl.multiple_of(side * half + part * piece, piece), piece)]
+        ref = gather_rows(way, step, part, side)
         return remote(ref, ref, share_send.at[way, step, part], share_recv.at[way, step, part], partner)
 
     def rotate(value, cosine, sine):
@@ -111,32 +114,35 @@
         swapped = jnp.where(lane < ROT_DIM // 2, pltpu.roll(value, LANES - ROT_DIM // 2, 1), pltpu.roll(value, ROT_DIM // 2, 1))
         return value * cosine + swapped * sine
 
-    def project(layer, way, step):
+    def turning(way, at):
+        cos_0, sin_0, cos_1, sin_1 = base_cos[at], base_sin[at], step_cos[way], step_sin[way]
+        lane = lax.broadcasted_iota(jnp.int32, (1, LANES), 1)
+        sign = jnp.where(lane < ROT_DIM // 2, -1.0, 1.0)
+        return cos_0 * cos_1 - sin_0 * sin_1, (sin_0 * cos_1 + cos_0 * sin_1) * sign
+
+    def project(layer, way, step, which):
+        cols = slice(which * width, (which + 1) * width)
+        return jnp.dot(hbuf[way, step], w_qkv[:, cols], preferred_element_type=F32) + b_qkv[layer, :, cols]
+
+    def project_kv(layer, way, step):
         for part in range(PARTS):
             share_copy(way, step, part, 1 - core).wait_recv()
         at = gathered_block(way, step)
-        normed = hbuf[way, at]
-        cos_0, sin_0, cos_1, sin_1 = base_cos[at], base_sin[at], step_cos[way], step_sin[way]
-        lane = lax.broadcasted_iota(jnp.int32, (1, LANES), 1)
-        sign = jnp.where(lane < ROT_DIM // 2, -1.0, 1.0)
-        cosine = cos_0 * cos_1 - sin_0 * sin_1
-        sine = (sin_0 * cos_1 + cos_0 * sin_1) * sign
-        for which, out in enumerate((q_all, k_all, v_all)):
-            cols = slice(which * width, (which + 1) * width)
-            proj = jnp.dot(normed, w_qkv[:, cols], preferred_element_type=F32) + b_qkv[layer, :, cols]
-            if which < 2:
-                for head in range(heads):
-                    lanes = slice(head * LANES, (head + 1) * LANES)
-                    turned = rotate(proj[:, lanes], cosine, sine)
-                    if which == 0:
-                        out[at, way, lanes] = turned.T.astype(BF16)
-                    else:
-                        out[at, way, :, lanes] = turned.astype(BF16)
-            else:
-                for head in range(heads):
-                    lanes = slice(head * LANES, (head + 1) * LANES)
-                    out[at, way, lanes] = proj[:, lanes].T.astype(BF16)
-        up = jnp.dot(normed, w_up[...], preferred_element_type=F32) + b_up[layer]
+        cosine, sine = turning(way, at)
+        keys, values = project(layer, way, step, 1), project(layer, way, step, 2)
+        for head in range(heads):
+            lanes = slice(head * LANES, (head + 1) * LANES)
+            k_all[at, way, :, lanes] = rotate(keys[:, lanes], cosine, sine).astype(BF16)
+            v_all[at, way, lanes] = values[:, lanes].T.astype(BF16)
+
+    def project_rest(layer, way, step):
+        at = gathered_block(way, step)
+        cosine, sine = turning(way, at)
+        queries = project(layer, way, step, 0)
+        for head in range(heads):
+            lanes = slice(head * LANES, (head + 1) * LANES)
+            q_all[at, way, lanes] = rotate(queries[:, lanes], cosine, sine).T.astype(BF16)
+        up = jnp.dot(hbuf[way, step], w_up[...], preferred_element_type=F32) + b_up[layer]
         m_all[at, way] = jax.nn.gelu(up, approximate=True).astype(BF16)
 
     def scattered_block(way, step):
@@ -177,7 +183,7 @@
             acc[way, slot, head] = acc[way, slot, head] * jnp.exp2(before - peak) + weighed
             top[way, slot, head] = peak
 
-    def attend_ahead(offset):
+    def attend_ahead(offset, units):
         block = ring_to_chip((pos + offset) % RING)
 
         def queries_of(unit, carry):
@@ -190,7 +196,7 @@
 
             return carry
 
-        lax.fori_loop(0, 4, queries_of, 0)
+        lax.fori_loop(0, units, queries_of, 0)
 
     def attended_by(way, step):
         at, slot = scattered_block(way, step), step % 2
@@ -204,6 +210,19 @@
                 return carry
 
             lax.fori_loop(0, at, body, 0)
+
+        @pl.when(step == 1)
+        def _():
+            def nearest(side, carry):
+                block = ring_to_chip((pos + 1 + side * (RING - 2)) % RING)
+
+                @pl.when(block < at)
+                def _():
+                    attend(way, slot, at, block, False)
+
+                return carry
+
+            lax.fori_loop(0, 2, nearest, 0)
 
         attend(way, slot, at, at, True)
         done = []
@@ -212,10 +231,29 @@
             done.append((sums / sums[head_dim:head_dim + 1]).T.astype(BF16))
         return jnp.concatenate(done, axis=1)
 
-    def contribute(way, step, before_send):
+    def both_sides(way, at):
+        return jnp.concatenate([m_all[at, way, mine], m_all[at, way, other]], axis=0)
+
+    def down_ahead(way):
+        up = both_sides(way, scattered_block(way, 0))
+        for low in range(0, depth, tile):
+            cols = slice(low, low + tile)
+            part_sum = jnp.dot(up, w_down[:, cols], preferred_element_type=F32)
+            own[way, 0, :, cols] = part_sum[:half]
+            own[way, 1, :, cols] = part_sum[half:]
+
+    def contribute_first(way):
+        attended = attended_by(way, 0)
+        for low in range(0, depth, tile):
+            cols = slice(low, low + tile)
+            part_sum = jnp.dot(attended, w_o[:, cols], preferred_element_type=F32)
+            own[way, 0, :, cols] = own[way, 0, :, cols] + part_sum[:half]
+            given[way, 0, :, cols] = (own[way, 1, :, cols] + part_sum[half:]).astype(BF16)
+
+    def contribute(way, step):
         at = scattered_block(way, step)
         attended = attended_by(way, step)
-        up = jnp.concatenate([m_all[at, way, mine], m_all[at, way, other]], axis=0)
+        up = both_sides(way, at)
 
         @pl.when(step >= 2)
         def _():
@@ -227,7 +265,6 @@
                         + jnp.dot(up, w_down[:, cols], preferred_element_type=F32))
             own[way, step % 2, :, cols] = part_sum[:half]
             given[way, step % 2, :, cols] = part_sum[half:].astype(BF16)
-        before_send()
         pair_copy(way, step).start()
 
     def total(way, step, part):
@@ -239,6 +276,7 @@
         for to in (right, left, partner):
             pl.semaphore_signal(ready.at[phase], inc=1, device_id={"tp": to}, device_id_type=MESH)
 
+    barrier = call(right, left, partner)
     for copy in in_copies(0):
         copy.start()
     for g in range(3 * heads):
@@ -261,24 +299,23 @@
                 low = which * width + head * LANES
                 b_qkv[layer, :, low:low + head_dim] = heads_f32[head:head + 1]
     out_ref[...] = x_ref[...]
-    meet(right, left, partner)
+    pl.semaphore_wait(barrier, 3)
 
     def layer_body(layer, carry):
         for copy in out_copies(layer):
             copy.start()
-        for way in range(2):
-            for part in range(PARTS):
-                low = way * half + part * piece
-                hbuf[way, chip, pl.ds(pl.multiple_of(core * half + part * piece, piece), piece)] = layer_norm(
-                    out_ref[low:low + piece], gain[layer], bias[layer])
-
-        @pl.when(layer > 0)
-        def _():
-            pl.semaphore_wait(ready.at[2 * layer - 1], 3)
-
         for part in range(PARTS):
             for way in range(2):
-                gather_copy(way, 0, 0, part).start()
+                low = way * half + part * piece
+                hbuf[way, 0, pl.ds(pl.multiple_of(core * half + part * piece, piece), piece)] = layer_norm(
+                    out_ref[low:low + piece], gain[layer], bias[layer])
+            if part == 0:
+                @pl.when(layer > 0)
+                def _():
+                    pl.semaphore_wait(ready.at[3 * layer - 1], 3)
+
+            for way in range(2):
+                gather_copy(way, 0, part).start()
                 share_copy(way, 0, part, core).start()
 
         for copy in in_copies(layer):
@@ -291,77 +328,92 @@
             for index in range(group):
                 part = event % 2 * group + index
                 for way in range(2):
-                    gather_copy(way, step, step - 1, part).wait_recv()
+                    gather_copy(way, step - 1, part).wait_recv()
 
                     @pl.when(step < RING - 1)
                     def _():
-                        gather_copy(way, step, step, part).start()
+                        gather_copy(way, step, part).start()
 
                     share_copy(way, step, part, core).start()
 
         def first_units(unit, carry):
-            project(layer, unit, 0)
+            project_kv(layer, unit, 0)
+            project_rest(layer, unit, 0)
             return carry
 
         def events(event, carry):
             arrive(event)
-            project(layer, (event + 1) % 2, (event + 1) // 2)
+            way, step = (event + 1) % 2, (event + 1) // 2
+            project_kv(layer, way, step)
+            project_rest(layer, way, step)
+
+            @pl.when(event == 4)
+            def _():
+                for copy in out_copies(layer):
+                    copy.wait()
+
+            @pl.when((event >= 4) & (event < 6))
+            def _():
+                down_ahead(event - 4)
 
             @pl.when(event >= RING)
             def _():
                 far, odd = (event - RING) // 2, event % 2
-                attend_ahead((1 - odd) * (RING // 2 - far) + odd * (RING // 2 + far) * ((far + 1) // 2))
-
+                attend_ahead((1 - odd) * (RING // 2 - far) + odd * (RING // 2 + far) * ((far + 1) // 2), 4)
+
+            return carry
+
+        def last_units(way, carry):
+            project_kv(layer, way, RING - 1)
             return carry
 
         def nearest(side, carry):
-            attend_ahead(1 + side * (RING - 2))
+            attend_ahead(1 + side * (RING - 2), 2)
             return carry
 
         for way in range(2):
             for slot in range(2):
                 fresh(way, slot)
-
         lax.fori_loop(0, 2, first_units, 0)
         arrive(0)
-        lax.fori_loop(1, 2 * RING - 2, events, 0)
-        project(layer, 1, RING - 1)
-        lax.fori_loop(0, 2, nearest, 0)
+        lax.fori_loop(1, 2 * RING - 3, events, 0)
+        attend_ahead(RING - 2, 4)
+        arrive(2 * RING - 3)
+        lax.fori_loop(0, 2, last_units, 0)
 
         def drain_gather(step, carry):
             for way in range(2):
                 for part in range(PARTS):
                     @pl.when(step < RING - 1)
                     def _():
-                        gather_copy(way, step, step, part).wait_send()
+                        gather_copy(way, step, part).wait_send()
 
                     share_copy(way, step, part, core).wait_send()
             return carry
 
         lax.fori_loop(0, RING, drain_gather, 0)
-        tell(2 * layer)
-
-        @pl.when(layer < layers - 1)
-        def _():
-            for copy in in_copies(layer + 1):
-                copy.start()
-
-        for copy in out_copies(layer):
-            copy.wait()
+        tell(3 * layer)
+        lax.fori_loop(0, 2, nearest, 0)
         for way in range(2):
             hbuf[way, 0, :half] = jnp.zeros((half, depth), BF16)
 
         def first_parts(way, carry):
-            def before_send():
-                @pl.when(way == 0)
-                def _():
-                    pl.semaphore_wait(ready.at[2 * layer], 3)
-
-            contribute(way, 0, before_send)
+            contribute_first(way)
+
+            @pl.when(way == 0)
+            def _():
+                pl.semaphore_wait(ready.at[3 * layer], 3)
+
+            pair_copy(way, 0).start()
             return carry
 
         def scatter_events(event, carry):
             step, second = event // 2, event % 2
+
+            @pl.when(event == 2 * RING - 4)
+            def _():
+                pl.semaphore_wait(ready.at[3 * layer + 1], 3)
+
             for index in range(group):
                 part = second * group + index
                 for way in range(2):
@@ -376,7 +428,21 @@
 
                     hbuf[way, step, span_of(part)] = total(way, step, part).astype(BF16)
                     scatter_copy(way, step, part).start()
-            contribute(second, step + 1, lambda: None)
+            contribute(second, step + 1)
+
+            @pl.when((event >= 1) & (event < 3))
+            def _():
+                project_rest(layer, event - 1, RING - 1)
+
+            @pl.when(event == 2)
+            def _():
+                tell(3 * layer + 1)
+
+                @pl.when(layer < layers - 1)
+                def _():
+                    for copy in in_copies(layer + 1):
+                        copy.start()
+
             return carry
 
         lax.fori_loop(0, 2, first_parts, 0)
@@ -403,7 +469,7 @@
 
         @pl.when(layer < layers - 1)
         def _():
-            tell(2 * layer + 1)
+            tell(3 * layer + 2)
 
         return carry
 
@@ -451,7 +517,7 @@
             pltpu.SemaphoreType.DMA((2, RING, PARTS)),
             pltpu.SemaphoreType.DMA((2, RING)),
             pltpu.SemaphoreType.DMA((2, RING)),
-            pltpu.SemaphoreType.REGULAR((2 * layers,)),
+            pltpu.SemaphoreType.REGULAR((3 * layers,)),
         ],
         compiler_params=pltpu.CompilerParams(collective_id=0, has_side_effects=True, vmem_limit_bytes=VMEM_LIMIT),
         name="layers",

time: 468 us -> 456 us (0.974)
  Pallas kernels: 462 us -> 451 us
    pallas_call x1, Pallas kernels: 462 us -> 451 us  [run_layers(): pl.pallas_call(layers_kernel, out_shape=jax.ShapeDtypeStruct((rows, depth...]
where the time goes in v5:
time: 456 us
  Pallas kernels  451 us (99%)
    pallas_call x1, Pallas kernels, run_layers(): pl.pallas_call(layers_kernel, out_shape=jax.ShapeDtypeStruct((rows, depth...  451 us

profile of v5, /device:TPU:0, one launch (start us, length us, event | category | flops | bytes accessed | tf_op | source)
XLA Modules:
  0.0 455.8 jit_solution(5637765743605802270)
XLA Ops:
  0.0 0.1 iota_bitcast_fusion
  0.1 0.1 add_convert_fusion
  0.2 0.1 mul.107
  0.3 0.7 multiply_sine_fusion.1
  1.0 1.8 multiply_sine_fusion
  2.8 450.5 %layers.1 = bf16[256,2560]{1,0:T(8,128)(2,1)} custom-call(bf16[256,2560]{1,0:T(8,128)(2,1)} %bitcast.14, bf16[2,2,80,2560]{3,2,1,0:T(8,128)(2,1)} %bitcast.11, bf16[2,2,80,2560]{3,2,1,0:T(8,128)(2,1)} %bitcast.12, bf16[2,2,80,2560]{3,2,1,0:T(8,128)(2,1)} %bitcast.13, bf16[2,2,80,2560]{3,2,1,0:T(8,128)(2,1)} %wo_hbm.1, bf16[2,2560,640]{2,1,0:T(8,128)(2,1)} %wup_hbm.1, ...), custom_call_target="tpu_custom_call" | custom-call | tf_op jit(solution)/shard_map/layers/pallas_call | solution.py:486
  453.3 2.5 copy.18
  (4 shorter events, 0.0 us)

commit v6 on v5

--- a/solution.py
+++ b/solution.py
@@ -58,13 +58,13 @@
     return (centered * lax.rsqrt(variance + LN_EPS) * gain + bias).astype(BF16)
 
 
-def layers_kernel(x_ref, wq_hbm, wk_hbm, wv_hbm, wo_hbm, wup_hbm, wdown_hbm, bq_ref, bk_ref, bv_ref, bup_ref, bo_ref, bdown_ref,
-                  gain_ref, bias_ref, base_cos, base_sin, step_cos, step_sin, out_ref,
-                  b_qkv, b_up, b_sum, gain, bias, hbuf, q_all, k_all, v_all, m_all, staged, w_qkv, w_up, w_o, w_down, given, own, acc, top,
+def layers_kernel(x_hbm, wq_hbm, wk_hbm, wv_hbm, wo_hbm, wup_hbm, wdown_hbm, bq_ref, bk_ref, bv_ref, bup_ref, bo_ref, bdown_ref,
+                  gain_ref, bias_ref, freq_ref, out_hbm,
+                  kept, base_cos, base_sin, step_cos, step_sin, b_qkv, b_up, b_sum, gain, bias, hbuf, q_all, k_all, v_all, m_all, staged, w_qkv, w_up, w_o, w_down, given, own, acc, top,
                   weight_sem, gather_send, gather_recv, share_send, share_recv,
-                  scatter_send, scatter_recv, pair_send, pair_recv, ready):
+                  scatter_send, scatter_recv, pair_send, pair_recv, ready, edge_sem):
     layers, heads, head_dim, depth = wq_hbm.shape
-    rows = x_ref.shape[0]
+    rows = x_hbm.shape[0]
     half = rows // 2
     piece = half // PARTS
     group = PARTS // 2
@@ -272,10 +272,16 @@
         taken = pl.ds(pl.multiple_of(half + part * piece, piece), piece)
         return own[way, step % 2, span] + hbuf[way, step, taken].astype(F32) + hbuf[way, step, span].astype(F32)
 
+    def out_copy(way, part):
+        span = pl.ds(way * half + part * piece, piece)
+        return pltpu.make_async_copy(kept.at[span], out_hbm.at[span], edge_sem.at[1 + way * PARTS + part])
+
     def tell(phase):
         for to in (right, left, partner):
             pl.semaphore_signal(ready.at[phase], inc=1, device_id={"tp": to}, device_id_type=MESH)
 
+    x_copy = pltpu.make_async_copy(x_hbm, kept, edge_sem.at[0])
+    x_copy.start()
     barrier = call(right, left, partner)
     for copy in in_copies(0):
         copy.start()
@@ -298,7 +304,7 @@
             for head in range(heads):
                 low = which * width + head * LANES
                 b_qkv[layer, :, low:low + head_dim] = heads_f32[head:head + 1]
-    out_ref[...] = x_ref[...]
+    x_copy.wait()
     pl.semaphore_wait(barrier, 3)
 
     def layer_body(layer, carry):
@@ -308,7 +314,7 @@
             for way in range(2):
                 low = way * half + part * piece
                 hbuf[way, 0, pl.ds(pl.multiple_of(core * half + part * piece, piece), piece)] = layer_norm(
-                    out_ref[low:low + piece], gain[layer], bias[layer])
+                    kept[low:low + piece], gain[layer], bias[layer])
             if part == 0:
                 @pl.when(layer > 0)
                 def _():
@@ -317,6 +323,21 @@
             for way in range(2):
                 gather_copy(way, 0, part).start()
                 share_copy(way, 0, part, core).start()
+
+        @pl.when(layer == 0)
+        def _():
+            chips = lax.broadcasted_iota(jnp.int32, (RING, 1), 0) * (2 * rows)
+            angle = chips.astype(F32) * freq_ref[...]
+            cosine, sine = jnp.cos(angle), jnp.sin(angle)
+            for at in range(RING):
+                base_cos[at] = cosine[at:at + 1]
+                base_sin[at] = sine[at:at + 1]
+            row = lax.broadcasted_iota(jnp.int32, (rows, 1), 0)
+            for way in range(2):
+                offset = (row // half) * rows + way * half + row % half
+                angle = offset.astype(F32) * freq_ref[...]
+                step_cos[way] = jnp.cos(angle)
+                step_sin[way] = jnp.sin(angle)
 
         for copy in in_copies(layer):
             copy.wait()
@@ -453,8 +474,13 @@
                     pair_copy(way, RING - 1).wait_recv()
                 scatter_copy(way, RING - 2, part).wait_recv()
                 low = way * half + part * piece
-                hidden = out_ref[low:low + piece].astype(F32) + total(way, RING - 1, part) + b_sum[layer]
-                out_ref[low:low + piece] = hidden.astype(BF16)
+                hidden = kept[low:low + piece].astype(F32) + total(way, RING - 1, part) + b_sum[layer]
+                kept[low:low + piece] = hidden.astype(BF16)
+
+                @pl.when(layer == layers - 1)
+                def _():
+                    out_copy(way, part).start()
+
 
         def drain_scatter(step, carry):
             for way in range(2):
@@ -474,9 +500,12 @@
         return carry
 
     lax.fori_loop(0, layers, layer_body, 0)
-
-
-def run_layers(x, w_q, w_k, w_v, w_o, w_up, w_down, vectors, tables):
+    for part in range(PARTS):
+        for way in range(2):
+            out_copy(way, part).wait()
+
+
+def run_layers(x, w_q, w_k, w_v, w_o, w_up, w_down, vectors, freq):
     rows, depth = x.shape
     layers, heads, head_dim, _ = w_q.shape
     width, hidden_width = heads * LANES, w_up.shape[2]
@@ -486,9 +515,14 @@
     return pl.pallas_call(
         layers_kernel,
         out_shape=jax.ShapeDtypeStruct((rows, depth), BF16),
-        in_specs=[vmem] + [hbm] * 6 + [vmem] * 12,
-        out_specs=vmem,
+        in_specs=[hbm] * 7 + [vmem] * 9,
+        out_specs=hbm,
         scratch_shapes=[
+            pltpu.VMEM((rows, depth), BF16),
+            pltpu.VMEM((RING, 1, LANES), F32),
+            pltpu.VMEM((RING, 1, LANES), F32),
+            pltpu.VMEM((2, rows, LANES), F32),
+            pltpu.VMEM((2, rows, LANES), F32),
             pltpu.VMEM((layers, 1, 3 * width), F32),
             pltpu.VMEM((layers, 1, hidden_width), F32),
             pltpu.VMEM((layers, 1, depth), F32),
@@ -518,21 +552,17 @@
             pltpu.SemaphoreType.DMA((2, RING)),
             pltpu.SemaphoreType.DMA((2, RING)),
             pltpu.SemaphoreType.REGULAR((3 * layers,)),
+            pltpu.SemaphoreType.DMA((1 + 2 * PARTS,)),
         ],
         compiler_params=pltpu.CompilerParams(collective_id=0, has_side_effects=True, vmem_limit_bytes=VMEM_LIMIT),
         name="layers",
-    )(x, w_q, w_k, w_v, w_o, w_up, w_down, *vectors, *tables)
-
-
-def rotary_tables(rows):
-    half = rows // 2
-    way, core, row = jnp.meshgrid(jnp.arange(2), jnp.arange(2), jnp.arange(half), indexing="ij")
-    offset = (core * rows + way * half + row).astype(F32).reshape(2, rows, 1)
-    base = (jnp.arange(RING, dtype=F32) * (2 * rows)).reshape(RING, 1, 1)
+    )(x, w_q, w_k, w_v, w_o, w_up, w_down, *vectors, freq)
+
+
+def rotary_frequencies():
     lane = jnp.arange(LANES)
     pair = (lane % (ROT_DIM // 2)).astype(F32)
-    inv_freq = jnp.where(lane < ROT_DIM, 1.0 / (ROPE_BASE ** (pair * (2.0 / ROT_DIM))), 0.0)
-    return jnp.cos(base * inv_freq), jnp.sin(base * inv_freq), jnp.cos(offset * inv_freq), jnp.sin(offset * inv_freq)
+    return jnp.where(lane < ROT_DIM, 1.0 / (ROPE_BASE ** (pair * (2.0 / ROT_DIM))), 0.0).reshape(1, LANES)
 
 
 def solution(mesh):
@@ -546,7 +576,7 @@
             return jnp.transpose(weight, (0, 2, 3, 1))
 
         out = run_layers(x_loc[0], heads_first(w_q), heads_first(w_k), heads_first(w_v), w_o, w_up, w_down,
-                         (b_q, b_k, b_v, b_up, b_o, b_down, ln_gain, ln_bias), rotary_tables(x_loc.shape[1]))
+                         (b_q, b_k, b_v, b_up, b_o, b_down, ln_gain, ln_bias), rotary_frequencies())
         return out[None]
 
     return jax.shard_map(local_program, mesh=mesh, in_specs=in_specs, out_specs=P("dp", "tp", None), check_vma=False)

time: 456 us -> 452 us (level)
  no operation moved by 1% of the time
where the time goes in v6:
time: 452 us; the launch traced here: 451 us
  Pallas kernels  448 us (99%)
    pallas_call x1, Pallas kernels, run_layers(): pl.pallas_call(layers_kernel, out_shape=jax.ShapeDtypeStruct((rows, depth...  448 us

profile of v6, /device:TPU:0, one launch (start us, length us, event | category | flops | bytes accessed | tf_op | source)
XLA Modules:
  0.0 451.2 jit_solution(3035799143248253483)
XLA Ops:
  0.0 0.5 compare_select_fusion.freq_ref
  0.5 448.3 %layers.1 = bf16[256,2560]{1,0:T(8,128)(2,1)} custom-call(bf16[256,2560]{1,0:T(8,128)(2,1)} %bitcast.9, bf16[2,2,80,2560]{3,2,1,0:T(8,128)(2,1)} %bitcast.6, bf16[2,2,80,2560]{3,2,1,0:T(8,128)(2,1)} %bitcast.7, bf16[2,2,80,2560]{3,2,1,0:T(8,128)(2,1)} %bitcast.8, bf16[2,2,80,2560]{3,2,1,0:T(8,128)(2,1)} %wo_hbm.1, bf16[2,2560,640]{2,1,0:T(8,128)(2,1)} %wup_hbm.1, ...), custom_call_target="tpu_custom_call" | custom-call | tf_op jit(solution)/shard_map/layers/pallas_call | solution.py:515
  448.8 2.5 copy.17

commit v7 on v6

--- a/solution.py
+++ b/solution.py
@@ -282,6 +282,16 @@
 
     x_copy = pltpu.make_async_copy(x_hbm, kept, edge_sem.at[0])
     x_copy.start()
+    def launch(layer, part, before_send):
+        for way in range(2):
+            low = way * half + part * piece
+            hbuf[way, 0, pl.ds(pl.multiple_of(core * half + part * piece, piece), piece)] = layer_norm(
+                kept[low:low + piece], gain[layer], bias[layer])
+        before_send()
+        for way in range(2):
+            gather_copy(way, 0, part).start()
+            share_copy(way, 0, part, core).start()
+
     barrier = call(right, left, partner)
     for copy in in_copies(0):
         copy.start()
@@ -306,23 +316,12 @@
                 b_qkv[layer, :, low:low + head_dim] = heads_f32[head:head + 1]
     x_copy.wait()
     pl.semaphore_wait(barrier, 3)
+    for part in range(PARTS):
+        launch(0, part, lambda: None)
 
     def layer_body(layer, carry):
         for copy in out_copies(layer):
             copy.start()
-        for part in range(PARTS):
-            for way in range(2):
-                low = way * half + part * piece
-                hbuf[way, 0, pl.ds(pl.multiple_of(core * half + part * piece, piece), piece)] = layer_norm(
-                    kept[low:low + piece], gain[layer], bias[layer])
-            if part == 0:
-                @pl.when(layer > 0)
-                def _():
-                    pl.semaphore_wait(ready.at[3 * layer - 1], 3)
-
-            for way in range(2):
-                gather_copy(way, 0, part).start()
-                share_copy(way, 0, part, core).start()
 
         @pl.when(layer == 0)
         def _():
@@ -396,6 +395,11 @@
             for slot in range(2):
                 fresh(way, slot)
         lax.fori_loop(0, 2, first_units, 0)
+
+        @pl.when(layer > 0)
+        def _():
+            pl.semaphore_wait(ready.at[4 * layer - 1], 3)
+
         arrive(0)
         lax.fori_loop(1, 2 * RING - 3, events, 0)
         attend_ahead(RING - 2, 4)
@@ -413,7 +417,7 @@
             return carry
 
         lax.fori_loop(0, RING, drain_gather, 0)
-        tell(3 * layer)
+        tell(4 * layer)
         lax.fori_loop(0, 2, nearest, 0)
         for way in range(2):
             hbuf[way, 0, :half] = jnp.zeros((half, depth), BF16)
@@ -423,7 +427,7 @@
 
             @pl.when(way == 0)
             def _():
-                pl.semaphore_wait(ready.at[3 * layer], 3)
+                pl.semaphore_wait(ready.at[4 * layer], 3)
 
             pair_copy(way, 0).start()
             return carry
@@ -433,7 +437,7 @@
 
             @pl.when(event == 2 * RING - 4)
             def _():
-                pl.semaphore_wait(ready.at[3 * layer + 1], 3)
+                pl.semaphore_wait(ready.at[4 * layer + 1], 3)
 
             for index in range(group):
                 part = second * group + index
@@ -457,7 +461,7 @@
 
             @pl.when(event == 2)
             def _():
-                tell(3 * layer + 1)
+                tell(4 * layer + 1)
 
                 @pl.when(layer < layers - 1)
                 def _():
@@ -468,6 +472,18 @@
 
         lax.fori_loop(0, 2, first_parts, 0)
         lax.fori_loop(0, 2 * RING - 2, scatter_events, 0)
+        def drain_scatter(step, carry):
+            for way in range(2):
+                for part in range(PARTS):
+                    scatter_copy(way, step, part).wait_send()
+            return carry
+
+        lax.fori_loop(0, 2, drain_scatter, 0)
+
+        @pl.when(layer < layers - 1)
+        def _():
+            tell(4 * layer + 2)
+
         for part in range(PARTS):
             for way in range(2):
                 if part == 0:
@@ -481,21 +497,22 @@
                 def _():
                     out_copy(way, part).start()
 
-
-        def drain_scatter(step, carry):
-            for way in range(2):
-                for part in range(PARTS):
-                    scatter_copy(way, step, part).wait_send()
-            return carry
-
-        lax.fori_loop(0, RING - 1, drain_scatter, 0)
+            @pl.when(layer < layers - 1)
+            def _():
+                def before_send():
+                    if part == 0:
+                        pl.semaphore_wait(ready.at[4 * layer + 2], 3)
+
+                launch(layer + 1, part, before_send)
+
+        lax.fori_loop(2, RING - 1, drain_scatter, 0)
         for way in range(2):
             for step in (RING - 2, RING - 1):
                 pair_copy(way, step).wait_send()
 
         @pl.when(layer < layers - 1)
         def _():
-            tell(3 * layer + 2)
+            tell(4 * layer + 3)
 
         return carry
 
@@ -551,7 +568,7 @@
             pltpu.SemaphoreType.DMA((2, RING, PARTS)),
             pltpu.SemaphoreType.DMA((2, RING)),
             pltpu.SemaphoreType.DMA((2, RING)),
-            pltpu.SemaphoreType.REGULAR((3 * layers,)),
+            pltpu.SemaphoreType.REGULAR((4 * layers,)),
             pltpu.SemaphoreType.DMA((1 + 2 * PARTS,)),
         ],
         compiler_params=pltpu.CompilerParams(collective_id=0, has_side_effects=True, vmem_limit_bytes=VMEM_LIMIT),

time: 452 us -> 447 us (0.989)
  no operation moved by 1% of the time
where the time goes in v7:
time: 447 us
  Pallas kernels  444 us (99%)
    pallas_call x1, Pallas kernels, run_layers(): pl.pallas_call(layers_kernel, out_shape=jax.ShapeDtypeStruct((rows, depth...  444 us

profile of v7, /device:TPU:0, one launch (start us, length us, event | category | flops | bytes accessed | tf_op | source)
XLA Modules:
  0.0 446.8 jit_solution(70130893399229254)
XLA Ops:
  0.0 0.5 compare_select_fusion.freq_ref
  0.5 443.8 %layers.1 = bf16[256,2560]{1,0:T(8,128)(2,1)} custom-call(bf16[256,2560]{1,0:T(8,128)(2,1)} %bitcast.9, bf16[2,2,80,2560]{3,2,1,0:T(8,128)(2,1)} %bitcast.6, bf16[2,2,80,2560]{3,2,1,0:T(8,128)(2,1)} %bitcast.7, bf16[2,2,80,2560]{3,2,1,0:T(8,128)(2,1)} %bitcast.8, bf16[2,2,80,2560]{3,2,1,0:T(8,128)(2,1)} %wo_hbm.1, bf16[2,2560,640]{2,1,0:T(8,128)(2,1)} %wup_hbm.1, ...), custom_call_target="tpu_custom_call" | custom-call | tf_op jit(solution)/shard_map/layers/pallas_call | solution.py:532
  444.3 2.5 copy.17
